TPU v7x, 8 devices: a whole 2x2x1 slice. The times are simulated.
8 devices in a mesh: dp: 2 (over z, y), sp: 4 (over x, core).
Axes of the slice: x: 2, y: 2, z: 1, core: 2. Of those that a mesh axis runs over, the one named last changes fastest.
Arguments:
- hidden: bfloat16 [256, 2048], P('dp'), parts along dimension 0
- ln_gamma: float32 [2048], replicated
- ln_beta: float32 [2048], replicated
- w_qkv: bfloat16 [2048, 2304], replicated
- w_out: bfloat16 [2048, 2048], replicated
- w_up: bfloat16 [2048, 8192], P(None, 'sp')
- w_down: bfloat16 [8192, 2048], P('sp')
- k_cache: bfloat16 [256, 2048, 128], P('dp', 'sp'), parts along dimension 0
- v_cache: bfloat16 [256, 2048, 128], P('dp', 'sp'), parts along dimension 0
- positions: int32 [256], P('dp'), parts along dimension 0
Outputs:
- output 1: bfloat16 [256, 2048], P('dp'), parts along dimension 0
- output 2: bfloat16 [256, 2048, 128], P('dp', 'sp'), parts along dimension 0
- output 3: bfloat16 [256, 2048, 128], P('dp', 'sp'), parts along dimension 0
There are 2 independent parts. A program takes and returns all parts, laid end to end along the dimension named above; an argument that names none is the same for every part.
All inputs are finite; a program needn't handle non-finite values.
Results may differ from a plain program's by a relative error of at most 0.00479244.
Values sent between devices are 32-bit elements.
A program may use at most 1 GiB of HBM per device.

v0:
```python
import jax
import jax.numpy as jnp
from jax import lax
from jax.sharding import PartitionSpec as P

LN_EPS = 1e-5
ROPE_BASE = 10000.0
NEG_FILL = -1e30


def layer_norm(hidden, ln_gamma, ln_beta):
    hidden_f32 = hidden.astype(jnp.float32)
    row_mean = jnp.mean(hidden_f32, axis=-1, keepdims=True)
    centered = hidden_f32 - row_mean
    row_var = jnp.mean(centered * centered, axis=-1, keepdims=True)
    return (centered * lax.rsqrt(row_var + LN_EPS) * ln_gamma + ln_beta).astype(jnp.bfloat16)


def rotary_tables(positions, head_dim):
    inv_freq = 1.0 / (ROPE_BASE ** (jnp.arange(0, head_dim, 2, dtype=jnp.float32) / head_dim))
    angles = positions.astype(jnp.float32)[:, None] * inv_freq[None, :]
    cos_half = jnp.cos(angles)
    sin_half = jnp.sin(angles)
    return jnp.concatenate([cos_half, cos_half], axis=-1), jnp.concatenate([sin_half, sin_half], axis=-1)


def apply_rotary(vecs, cos_full, sin_full):
    vecs_f32 = vecs.astype(jnp.float32)
    half_dim = vecs.shape[-1] // 2
    rotated = jnp.concatenate([-vecs_f32[..., half_dim:], vecs_f32[..., :half_dim]], axis=-1)
    return (vecs_f32 * cos_full + rotated * sin_full).astype(jnp.bfloat16)


def local_stats(q_rot, k_block, v_block, local_pos):
    head_dim = q_rot.shape[-1]
    slot_ids = jnp.arange(k_block.shape[1])
    scores = jnp.einsum('bhd,bsd->bhs', q_rot, k_block, preferred_element_type=jnp.float32) * head_dim ** -0.5
    valid_mask = (slot_ids[None, :] <= local_pos[:, None])[:, None, :]
    masked = jnp.where(valid_mask, scores, NEG_FILL)
    block_max = jnp.max(masked, axis=-1)
    exp_scores = jnp.where(valid_mask, jnp.exp(masked - block_max[..., None]), 0.0)
    block_sum = jnp.sum(exp_scores, axis=-1)
    block_ctx = jnp.einsum('bhs,bsd->bhd', exp_scores.astype(jnp.bfloat16), v_block, preferred_element_type=jnp.float32)
    return jnp.concatenate([block_ctx, block_max[..., None], block_sum[..., None]], axis=-1)


def combine_stats(all_stats):
    head_dim = all_stats.shape[-1] - 2
    block_max = all_stats[..., head_dim]
    top_max = jnp.max(block_max, axis=0)
    scale_w = jnp.exp(block_max - top_max[None])
    total_sum = jnp.sum(all_stats[..., head_dim + 1] * scale_w, axis=0)
    total_ctx = jnp.sum(all_stats[..., :head_dim] * scale_w[..., None], axis=0)
    return (total_ctx / total_sum[..., None]).astype(jnp.bfloat16)


def device_step(hidden, ln_gamma, ln_beta, w_qkv, w_out, w_up, w_down, k_cache, v_cache, positions):
    batch_rows = hidden.shape[0]
    seq_dev, head_dim = k_cache.shape[1], k_cache.shape[2]
    num_heads = w_out.shape[0] // head_dim
    normed = layer_norm(hidden, ln_gamma, ln_beta)
    qkv_proj = jnp.dot(normed, w_qkv, preferred_element_type=jnp.float32).astype(jnp.bfloat16)
    qkv_proj = qkv_proj.reshape(batch_rows, num_heads + 2, head_dim)
    cos_full, sin_full = rotary_tables(positions, head_dim)
    q_rot = apply_rotary(qkv_proj[:, :num_heads], cos_full[:, None, :], sin_full[:, None, :])
    k_rot = apply_rotary(qkv_proj[:, num_heads], cos_full, sin_full)
    v_new = qkv_proj[:, num_heads + 1]
    local_pos = positions - lax.axis_index('sp') * seq_dev
    write_mask = (jnp.arange(seq_dev)[None, :] == local_pos[:, None])[:, :, None]
    k_next = jnp.where(write_mask, k_rot[:, None, :], k_cache)
    v_next = jnp.where(write_mask, v_new[:, None, :], v_cache)
    block_stats = local_stats(q_rot, k_next, v_next, local_pos)
    all_stats = lax.all_gather(block_stats, 'sp')
    context = combine_stats(all_stats).reshape(batch_rows, num_heads * head_dim)
    attn_out = jnp.dot(context, w_out, preferred_element_type=jnp.float32)
    up_proj = jnp.dot(normed, w_up, preferred_element_type=jnp.float32)
    activated = jax.nn.gelu(up_proj, approximate=False).astype(jnp.bfloat16)
    mlp_part = jnp.dot(activated, w_down, preferred_element_type=jnp.float32)
    mlp_out = lax.psum(mlp_part, 'sp')
    out_hidden = (hidden.astype(jnp.float32) + attn_out + mlp_out).astype(jnp.bfloat16)
    return out_hidden, k_next, v_next


def solution(mesh):
    cache_spec = P('dp', 'sp', None)
    in_specs = (P('dp', None), P(None), P(None), P(None, None), P(None, None), P(None, 'sp'), P('sp', None), cache_spec, cache_spec, P('dp'))
    out_specs = (P('dp', None), cache_spec, cache_spec)
    return jax.shard_map(device_step, mesh=mesh, in_specs=in_specs, out_specs=out_specs, check_vma=False)
```

profile of v0, /device:TPU:0, one launch (start us, length us, event | category | flops | bytes accessed | tf_op | source)
XLA Modules:
  0.0 152.8 jit_solution(13363028890684663925)
XLA Ops:
  7.2 0.7 broadcast_subtract_fusion
  8.4 1.2 convert_reduce_fusion
  9.6 1.3 fusion.15
  10.9 5.4 %convolution_convert_fusion = bf16[128,2304]{1,0:T(8,128)(2,1)S(1)} fusion(bf16[2048,2304]{1,0:T(8,128)(2,1)} %param.13, bf16[128,2048]{1,0:T(8,128)(2,1)} %param.10, f32[2048]{0:T(1024)} %param.12, f32[2048]{0:T(1024)} %param.11, f32[128]{0:T(128)S(1)} %add_rsqrt_fusion, f32[128]{0:T(128)S(1)} %broadcast_multiply_fusion), kind=kOutput, calls=%fused_computation.7 | convolution fusion | flops 1209827328 | bytes 10568704 | tf_op jit(solution)/shard_map/dot_general | solution.py:62
  16.3 0.3 copy.60
  17.5 0.4 copy.62
  17.9 23.3 %broadcast_select_fusion = (bf16[128,512,128]{2,1,0:T(8,128)(2,1)}, bf16[128,512,128]{2,1,0:T(8,128)(2,1)}) fusion(bf16[128,512,128]{2,1,0:T(8,128)(2,1)} %param.18, pred[128,512]{1,0:T(8,128)(4,1)S(1)} %get-tuple-element.15, bf16[128,128]{1,0:T(8,128)(2,1)S(1)} %bitcast.46, bf16[128,512,128]{2,1,0:T(8,128)(2,1)} %param.17, bf16[128,128]{1,0:T(8,128)(2,1)S(1)} %copy.61), kind=kLoop, calls=%fused_computation | loop fusion | flops 16777216 | bytes 67239936 | tf_op jit(solution)/shard_map/jit(_where)/select_n | solution.py:71
  41.2 12.2 %fusion.1 = (f32[128,16]{1,0:T(8,128)S(1)}, f32[128,16,512]{2,1,0:T(8,128)}) fusion(pred[128,512]{1,0:T(8,128)(4,1)S(1)} %get-tuple-element.14, bf16[128,16,128]{2,1,0:T(8,128)(2,1)S(1)} %copy.62, bf16[128,512,128]{2,1,0:T(8,128)(2,1)} %get-tuple-element.8), kind=kOutput, calls=%fused_computation.6 | convolution fusion | flops 271579136 | bytes 21569536 | tf_op jit(solution)/shard_map/bhd,bsd->bhs/dot_general | solution.py:37
  53.3 3.5 %fusion.2 = f32[128,16]{1,0:T(8,128)S(1)} fusion(f32[128,16,512]{2,1,0:T(8,128)} %get-tuple-element.19, f32[128,16]{1,0:T(8,128)S(1)} %get-tuple-element.18, pred[128,512]{1,0:T(8,128)(4,1)S(1)} %get-tuple-element.14), kind=kLoop, calls=%fused_computation.8 | loop fusion | flops 5240832 | bytes 4276224 | tf_op jit(solution)/shard_map/reduce_sum | solution.py:42
  56.9 7.3 %fusion.6 = f32[128,16,128]{2,1,0:T(8,128)S(1)} fusion(bf16[128,512,128]{2,1,0:T(8,128)(2,1)} %get-tuple-element.7, f32[128,16,512]{2,1,0:T(8,128)S(1)} %copy-done, f32[128,16]{1,0:T(8,128)S(1)} %get-tuple-element.18, pred[128,512]{1,0:T(8,128)(4,1)S(1)} %get-tuple-element.14), kind=kOutput, calls=%fused_computation.13 | convolution fusion | flops 273678336 | bytes 22093824 | tf_op jit(solution)/shard_map/bhs,bsd->bhd/dot_general | solution.py:43
  64.2 1.8 %copy.67 = f32[128,16,1]{2,1,0:T(8,128)} copy(f32[128,16,1]{1,0,2:T(8,128)S(1)} %bitcast.45) | data formatting | bytes 16384 | tf_op jit(solution)/shard_map/broadcast_in_dim | solution.py:44
  66.0 1.9 %copy.66 = f32[128,16,1]{2,1,0:T(8,128)} copy(f32[128,16,1]{1,0,2:T(8,128)S(1)} %bitcast.44) | data formatting | bytes 16384 | tf_op jit(solution)/shard_map/broadcast_in_dim | solution.py:41
  67.8 2.0 %pad_maximum_fusion = f32[128,16,130]{2,1,0:T(8,128)S(1)} fusion(f32[128,16,1]{2,1,0:T(8,128)} %copy.67, f32[128,16,1]{2,1,0:T(8,128)} %copy.66, f32[128,16,128]{2,1,0:T(8,128)S(1)} %fusion.6), kind=kLoop, calls=%fused_computation.14 | loop fusion | flops 532480 | bytes 2129920 | tf_op jit(solution)/shard_map/concatenate | solution.py:44
  69.8 1.8 %copy.68 = f32[128,16,130]{0,1,2:T(8,128)} copy(f32[128,16,130]{2,1,0:T(8,128)S(1)} %pad_maximum_fusion) | data formatting | bytes 2129920 | tf_op jit(solution)/shard_map/concatenate | solution.py:44
  71.6 0.2 all-reduce.2.cloned.1.call-start
  71.9 11.6 %fusion.31 = f32[128,2048]{1,0:T(8,128)} fusion(bf16[2048,2048]{1,0:T(8,128)(2,1)} %param.16, bf16[2048,2048]{1,0:T(8,128)(2,1)} %param.15, bf16[128,2048]{1,0:T(8,128)(2,1)} %param.10, f32[2048]{0:T(1024)S(1)} %copy-done.2, f32[2048]{0:T(1024)S(1)} %copy-done.3, f32[128]{0:T(128)S(1)} %add_rsqrt_fusion, f32[128]{0:T(128)S(1)} %broadcast_multiply_fusion), kind=kOutput, calls=%fused_computation.51 | convolution fusion | flops 2166095872 | bytes 18367488 | tf_op jit(solution)/shard_map/dot_general | solution.py:78
  83.6 23.5 %all-gather.3.cloned.1.call-done = f32[512,16,130]{0,1,2:T(8,128)} async-done(((f32[128,16,130]{0,1,2:T(8,128)}), f32[512,16,130]{0,1,2:T(8,128)}) %all-gather.3.cloned.1.call-update) | async-done | bytes 4259856 | tf_op jit(solution)/shard_map/all_gather | solution.py:73
  107.1 5.6 %reshape.201 = f32[4,128,16,130]{1,0,2,3:T(4,128)} reshape(f32[512,16,130]{0,1,2:T(8,128)} %all-gather.3.cloned.1.call-done) | data formatting | bytes 8519680 | tf_op jit(solution)/shard_map/all_gather | solution.py:73
  112.6 0.8 slice_reduce_fusion
  113.5 0.8 fusion.66
  114.3 0.8 exponential_bitcast_fusion
  115.1 5.2 %fusion = f32[128,16,128]{0,1,2:T(8,128)S(1)} fusion(f32[4,128,16,130]{1,0,2,3:T(4,128)} %reshape.201, f32[4,128,16]{1,0,2:T(4,128)S(1)} %exponential_bitcast_fusion), kind=kLoop, calls=%fused_computation.3 | loop fusion | flops 1835008 | bytes 5275648 | tf_op jit(solution)/shard_map/reduce_sum | solution.py:53
  120.6 19.7 %all-reduce.2.cloned.1.call-done = f32[128,2048]{1,0:T(8,128)} async-done(((f32[128,2048]{1,0:T(8,128)}), f32[128,2048]{1,0:T(8,128)}) %all-reduce.2.cloned.1.call-update) | async-done | bytes 1048592 | tf_op jit(solution)/shard_map/psum | solution.py:79
  140.3 5.7 %fusion.5 = bf16[128,2048]{1,0:T(8,128)(2,1)} fusion(f32[128,2048]{1,0:T(8,128)} %all-reduce.2.cloned.1.call-done, bf16[128,2048]{0,1:T(8,128)(2,1)S(1)} %bitcast.43, bf16[2048,2048]{1,0:T(8,128)(2,1)} %param.14, bf16[128,2048]{1,0:T(8,128)(2,1)S(1)} %copy-done.1), kind=kOutput, calls=%fused_computation.12 | convolution fusion | flops 1074790400 | bytes 11010048 | tf_op jit(solution)/shard_map/dot_general | solution.py:75
  (28 shorter events, 1.5 us)
Async XLA Ops:
  7.2 99.9 %all-gather.3.cloned.1.call-start = ((), (), s32[]{:S(2)}) async-start(), calls=%async_computation.1 | async-start | bytes 5324800 | tf_op jit(solution)/shard_map/all_gather | solution.py:73
  53.3 3.5 %copy-start = (f32[128,16,512]{2,1,0:T(8,128)S(1)}, f32[128,16,512]{2,1,0:T(8,128)}, u32[]{:S(2)}) copy-start(f32[128,16,512]{2,1,0:T(8,128)} %get-tuple-element.19) | copy-start | bytes 12582916
  67.8 4.0 %copy-start.2 = (f32[2048]{0:T(1024)S(1)}, f32[2048]{0:T(1024)}, u32[]{:S(2)}) copy-start(f32[2048]{0:T(1024)} %param.12) | copy-start | bytes 24580
  67.8 4.0 %copy-start.3 = (f32[2048]{0:T(1024)S(1)}, f32[2048]{0:T(1024)}, u32[]{:S(2)}) copy-start(f32[2048]{0:T(1024)} %param.11) | copy-start | bytes 24580
  71.6 68.6 %all-reduce.2.cloned.1.call-start = ((), (), s32[]{:S(2)}) async-start(), calls=%async_computation | async-start | bytes 2097152 | tf_op jit(solution)/shard_map/psum | solution.py:79
  112.6 27.6 %copy-start.1 = (bf16[128,2048]{1,0:T(8,128)(2,1)S(1)}, bf16[128,2048]{1,0:T(8,128)(2,1)}, u32[]{:S(2)}) copy-start(bf16[128,2048]{1,0:T(8,128)(2,1)} %param.10) | copy-start | bytes 1572868
Sparse Core Ops, SparseCore 0:
  71.8 35.2 all-gather.2
  109.4 30.8 all-reduce.1
where the time goes:
time: 153 us
  waiting for transfers between devices  43.2 us (28%)
  matrix products  42.2 us (28%)
  other arithmetic  40.8 us (27%)
  between operations  14.2 us (9%)
  local copies, waits for them, and re-layouts  12.1 us (8%)
    all_gather x1, waiting for transfers between devices, device_step(): all_stats = lax.all_gather(block_stats, 'sp')  23.5 us
    select_n x1, other arithmetic, device_step(): v_next = jnp.where(write_mask, v_new[:, None, :], v_cache)  23.3 us
    psum x1, waiting for transfers between devices, device_step(): mlp_out = lax.psum(mlp_part, 'sp')  19.7 us
    dot_general x1, matrix products, local_stats(): jnp.einsum('bhd,bsd->bhs', q_rot, k_block, preferred_element_type=jnp.flo...  12.2 us
    dot_general x1, matrix products, device_step(): mlp_part = jnp.dot(activated, w_down, preferred_element_type=jnp.float32)  11.6 us
    dot_general x1, matrix products, local_stats(): jnp.einsum('bhs,bsd->bhd', exp_scores.astype(jnp.bfloat16), v_block, pref...  7.31 us
    dot_general x1, matrix products, device_step(): attn_out = jnp.dot(context, w_out, preferred_element_type=jnp.float32)  5.69 us
    all_gather x1, local copies, waits for them, and re-layouts, device_step(): all_stats = lax.all_gather(block_stats, 'sp')  5.56 us
  transfers between devices with their start and end apart: 2, of which 2 were waited for; matrix products, arithmetic and copies ran while one was open for 16% of the time, Pallas kernels for 0%

commit v1 on v0

v1 whole, which is shorter than its diff:
```python
import jax
import jax.numpy as jnp
from jax import lax
from jax.experimental import pallas as pl
from jax.experimental.pallas import tpu as pltpu
from jax.sharding import PartitionSpec as P


MESH = pl.DeviceIdType.MESH
LN_EPS = 1e-5
ROPE_BASE = 10000.0
NEG_FILL = -1e30
HEAD_DIM = 128
BLK = 512
STEP_ROWS = 8
AHEAD = 6
GROUPS = (40, 40, 32, 16)
F32, BF16 = jnp.float32, jnp.bfloat16


def rope_tables(positions):
    inv_freq = 1.0 / (ROPE_BASE ** (jnp.arange(0, HEAD_DIM, 2, dtype=F32) / HEAD_DIM))
    angles = positions.astype(F32)[:, None] * inv_freq[None, :]
    cos_half, sin_half = jnp.cos(angles), jnp.sin(angles)
    return jnp.concatenate([cos_half, cos_half], axis=-1), jnp.concatenate([-sin_half, sin_half], axis=-1)


def layer_kernel(pos_ref, posv_ref, x_hbm, gamma_ref, beta_ref, cos_ref, sin_ref, wqkv_hbm, wup_hbm, wdown_hbm, wout_hbm,
                 k_hbm, v_hbm, kv_ref, mlp_ref, y_ref,
                 xbuf, hbuf, kvw, wbuf, q_s, kn_ref, vn_ref, act, ctx_ref, part, mrecv, arecv, s_loc, s_recv, chip_o, chip_ml, x_o, x_ml,
                 xsem, kvwsem, wsem, osem, ksem, vsem, q_ss, q_rs, m_ss, m_rs, c_ss, c_rs, o_ss, o_rs, t_ss, t_rs, a_ss, a_rs):
    dp, sp = lax.axis_index('dp'), lax.axis_index('sp')
    core = lax.rem(sp, 2)
    mate = (dp, sp + 1 - 2 * core)
    across = (dp, lax.rem(sp + 2, 4))
    rows = xbuf.shape[0]
    n_steps = rows // STEP_ROWS
    seq_dev = k_hbm.shape[1]
    half_heads = q_s.shape[2]
    half_cols = half_heads * HEAD_DIM
    scale = HEAD_DIM ** -0.5

    def weight_copy(src, col, slot, idx):
        return pltpu.make_async_copy(src.at[:, pl.ds(pl.multiple_of(col, BLK), BLK)], wbuf.at[slot], wsem.at[idx])

    def q_copy(j):
        return weight_copy(wqkv_hbm, core * half_cols + j * BLK, j, j)

    def up_copy(j):
        return weight_copy(wup_hbm, j * BLK, 2 + j, 2 + j)

    def down_copy(j):
        half = jnp.where(j < 2, 1 - core, core) if not isinstance(j, int) else ((1 - core) if j < 2 else core)
        return weight_copy(wdown_hbm, half * half_cols + lax.rem(j, 2) * BLK, j, 6 + j)

    def out_copy(j):
        half = (1 - core) if j < 2 else core
        src = wout_hbm.at[pl.ds(pl.multiple_of(core * half_cols, half_cols), half_cols),
                          pl.ds(pl.multiple_of(half * half_cols + (j % 2) * BLK, BLK), BLK)]
        return pltpu.make_async_copy(src, wbuf.at[4 + j // 2, pl.ds((j % 2) * half_cols, half_cols)], osem.at[j])

    def k_copy(i):
        r = pl.ds(i * STEP_ROWS, STEP_ROWS)
        return pltpu.make_async_copy(k_hbm.at[r], kv_ref.at[0, r], ksem.at[i])

    def v_copy(i):
        r = pl.ds(i * STEP_ROWS, STEP_ROWS)
        return pltpu.make_async_copy(v_hbm.at[r], kv_ref.at[1, r], vsem.at[i])

    def cache_start(i):
        k_copy(i).start()
        v_copy(i).start()

    x_copy = pltpu.make_async_copy(x_hbm, xbuf, xsem)
    x_copy.start()
    kvw_copy = pltpu.make_async_copy(wqkv_hbm.at[:, pl.ds(2 * half_cols, 2 * HEAD_DIM)], kvw, kvwsem)
    kvw_copy.start()
    for j in range(2):
        q_copy(j).start()
    for j in range(4):
        up_copy(j).start()

    barrier = pltpu.get_barrier_semaphore()
    for dev in (mate, across):
        pl.semaphore_signal(barrier, inc=1, device_id=dev, device_id_type=MESH)
    pl.semaphore_wait(barrier, 2)

    x_copy.wait()

    def norm_rows(i, _):
        r = pl.ds(pl.multiple_of(i * 16, 16), 16)
        h = xbuf[r, :].astype(F32)
        centered = h - jnp.mean(h, axis=-1, keepdims=True)
        var = jnp.mean(centered * centered, axis=-1, keepdims=True)
        hbuf[r, :] = (centered * lax.rsqrt(var + LN_EPS) * gamma_ref[...] + beta_ref[...]).astype(BF16)
        return 0

    lax.fori_loop(0, rows // 16, norm_rows, 0)

    def rotate(vec):
        vec = vec.astype(BF16).astype(F32)
        return (vec * cos_ref[...] + pltpu.roll(vec, HEAD_DIM // 2, 1) * sin_ref[...]).astype(BF16)

    kvw_copy.wait()
    kv_new = jnp.dot(hbuf[...], kvw[...], preferred_element_type=F32)
    k_new = rotate(kv_new[:, :HEAD_DIM])
    v_new = kv_new[:, HEAD_DIM:].astype(BF16)
    kn_ref[...] = k_new.astype(F32)
    vn_ref[...] = v_new.astype(F32)
    kv_ref[0, rows, 0:rows, :] = k_new
    kv_ref[1, rows, 0:rows, :] = v_new
    at = jnp.broadcast_to(posv_ref[...] - sp * seq_dev, (16, rows))
    tile = lax.shift_right_logical(jnp.clip(at, 0, seq_dev - 1), 4)
    inside = jnp.logical_and(at >= 0, at < seq_dev)
    kv_ref[0, rows, rows:rows + 16, :] = tile.astype(F32).astype(BF16)
    kv_ref[0, rows, rows + 16:rows + 32, :] = jnp.where(inside, at - tile * 16, 16).astype(F32).astype(BF16)

    for j in range(2):
        q_copy(j).wait()
        for n in range(2):
            q_part = jnp.dot(hbuf[...], wbuf[j, :, n * 256:(n + 1) * 256], preferred_element_type=F32)
            for t in range(2):
                q_s[core, :, j * 4 + n * 2 + t, :] = rotate(q_part[:, t * HEAD_DIM:(t + 1) * HEAD_DIM]).astype(F32)
        down_copy(j).start()
    q_send = pltpu.make_async_remote_copy(src_ref=q_s.at[core], dst_ref=q_s.at[core], send_sem=q_ss, recv_sem=q_rs,
                                          device_id=mate, device_id_type=MESH)
    q_send.start()

    def up_step(j, _):
        up_copy(j).wait()
        for n in range(2):
            up = jnp.dot(hbuf[...], wbuf[2 + j, :, n * 256:(n + 1) * 256], preferred_element_type=F32)
            gelu = 0.5 * up * (1.0 + lax.erf(up * (0.5 ** 0.5)))
            act[:, pl.ds(pl.multiple_of(j * BLK + n * 256, 256), 256)] = gelu.astype(BF16)

        @pl.when(j < 2)
        def _():
            down_copy(2 + j).start()

        @pl.when(j >= 2)
        def _():
            cache_start(j - 2)

        return 0

    lax.fori_loop(0, 4, up_step, 0)

    def down_step(j, _):
        down_copy(j).wait()
        for n in range(2):
            part[j // 2, :, pl.ds(pl.multiple_of(lax.rem(j, 2) * BLK + n * 256, 256), 256)] = jnp.dot(
                act[...], wbuf[j, :, n * 256:(n + 1) * 256], preferred_element_type=F32)
        cache_start(2 + j)
        return 0

    m_send = pltpu.make_async_remote_copy(src_ref=part.at[0], dst_ref=mrecv, send_sem=m_ss, recv_sem=m_rs,
                                          device_id=mate, device_id_type=MESH)
    lax.fori_loop(0, 2, down_step, 0)
    m_send.start()
    lax.fori_loop(2, 4, down_step, 0)
    q_send.wait()

    slots = lax.broadcasted_iota(jnp.int32, (2 * half_heads, seq_dev), 1)
    lanes = lax.broadcasted_iota(jnp.int32, (half_heads, 128), 1)
    zero_q = jnp.zeros((2 * half_heads, HEAD_DIM), BF16)

    def attend(i, _):
        k_copy(i).wait()
        v_copy(i).wait()

        @pl.when(i + AHEAD < n_steps)
        def _():
            cache_start(i + AHEAD)

        @pl.when(i == n_steps - AHEAD)
        def _():
            for j in range(4):
                out_copy(j).start()

        for pair in range(STEP_ROWS // 2):
            bs = [i * STEP_ROWS + 2 * pair + t for t in range(2)]
            qf = [jnp.concatenate([q_s[0, b], q_s[1, b]], axis=0) for b in bs]
            qb = [q.astype(BF16) for q in qf]
            lhs = jnp.concatenate([jnp.concatenate([qb[0], zero_q], axis=1), jnp.concatenate([zero_q, qb[1]], axis=1)], axis=0)
            k2 = jnp.concatenate([kv_ref[0, b] for b in bs], axis=1)
            s2 = lax.dot_general(lhs, k2, (((1,), (1,)), ((), ())), preferred_element_type=F32) * scale
            probs, stats = [], []
            for t, b in enumerate(bs):
                at = pos_ref[b] - sp * seq_dev
                s = s2[t * 2 * half_heads:(t + 1) * 2 * half_heads]
                old = slots < at
                here = jnp.logical_and(at >= 0, at < seq_dev)
                masked = jnp.where(old, s, NEG_FILL)
                s_new = jnp.sum(qf[t] * kn_ref[pl.ds(b, 1), :], axis=-1, keepdims=True) * scale
                s_new = jnp.where(here, s_new, NEG_FILL)
                m = jnp.maximum(jnp.max(masked, axis=-1, keepdims=True), s_new)
                e = jnp.where(old, jnp.exp(masked - m), 0.0)
                e_new = jnp.where(here, jnp.exp(s_new - m), 0.0)
                l = jnp.sum(e, axis=-1, keepdims=True) + e_new
                probs.append(e.astype(BF16))
                stats.append((m, l, e_new.astype(BF16).astype(F32) * vn_ref[pl.ds(b, 1), :]))
            v2 = jnp.concatenate([kv_ref[1, b] for b in bs], axis=1)
            o2 = jnp.dot(jnp.concatenate(probs, axis=0), v2, preferred_element_type=F32)
            for t, b in enumerate(bs):
                m, l, extra = stats[t]
                o = o2[t * 2 * half_heads:(t + 1) * 2 * half_heads, t * HEAD_DIM:(t + 1) * HEAD_DIM] + extra
                mb = jnp.broadcast_to(m, o.shape)
                lb = jnp.broadcast_to(l, o.shape)
                for f in range(2):
                    hs = slice(f * half_heads, (f + 1) * half_heads)
                    s_loc[f, b, 0] = o[hs]
                    s_loc[f, b, 1] = mb[hs]
                    s_loc[f, b, 2] = lb[hs]
        return 0

    starts = [sum(GROUPS[:g]) for g in range(len(GROUPS))]

    def swap_copy(g):
        r = pl.ds(starts[g], GROUPS[g])
        return pltpu.make_async_remote_copy(src_ref=s_loc.at[1 - core, r], dst_ref=s_recv.at[r], send_sem=c_ss.at[g],
                                            recv_sem=c_rs.at[g], device_id=mate, device_id_type=MESH)

    def cross_copies(g):
        r = pl.ds(starts[g], GROUPS[g])
        return (pltpu.make_async_remote_copy(src_ref=chip_o.at[r], dst_ref=x_o.at[r], send_sem=o_ss.at[g],
                                             recv_sem=o_rs.at[g], device_id=across, device_id_type=MESH),
                pltpu.make_async_remote_copy(src_ref=chip_ml.at[g], dst_ref=x_ml.at[g], send_sem=t_ss.at[g],
                                             recv_sem=t_rs.at[g], device_id=across, device_id_type=MESH))

    def merge_chip(g):
        swap_copy(g).wait()

        def body(i, tiles):
            tm, tl = tiles
            for u in range(8):
                b = starts[g] + i * 8 + u
                m_a, m_b = s_loc[core, b, 1], s_recv[b, 1]
                top = jnp.maximum(m_a, m_b)
                w_a, w_b = jnp.exp(m_a - top), jnp.exp(m_b - top)
                chip_o[b] = s_loc[core, b, 0] * w_a + s_recv[b, 0] * w_b
                total = s_loc[core, b, 2] * w_a + s_recv[b, 2] * w_b
                s_recv[b, 1] = top
                s_recv[b, 2] = total
                hit = lanes == i * 8 + u
                tm = jnp.where(hit, top, tm)
                tl = jnp.where(hit, total, tl)
            return tm, tl

        zero = jnp.zeros((half_heads, 128), F32)
        tm, tl = lax.fori_loop(0, GROUPS[g] // 8, body, (zero, zero))
        chip_ml[g, 0] = tm
        chip_ml[g, 1] = tl
        for copy in cross_copies(g):
            copy.start()

    def merge_all(g):
        for copy in cross_copies(g):
            copy.wait()
        tm, tl = x_ml[g, 0], x_ml[g, 1]

        def body(i, _):
            for u in range(8):
                b = starts[g] + i * 8 + u
                hit = lanes == i * 8 + u
                m_b = jnp.sum(jnp.where(hit, tm, 0.0), axis=-1, keepdims=True)
                l_b = jnp.sum(jnp.where(hit, tl, 0.0), axis=-1, keepdims=True)
                m_a = s_recv[b, 1]
                top = jnp.maximum(m_a, m_b)
                w_a, w_b = jnp.exp(m_a - top), jnp.exp(m_b - top)
                total = s_recv[b, 2] * w_a + l_b * w_b
                x_o[b] = (chip_o[b] * w_a + x_o[b] * w_b) / total
            return 0

        lax.fori_loop(0, GROUPS[g] // 8, body, 0)

    n_groups = len(GROUPS)
    for g in range(n_groups):
        lax.fori_loop(starts[g] // STEP_ROWS, (starts[g] + GROUPS[g]) // STEP_ROWS, attend, 0)
        swap_copy(g).start()
        if g == 0:
            m_send.wait()
            mlp_ref[...] = part[1] + mrecv[...]
        if g >= 1:
            merge_chip(g - 1)
        if g >= 2:
            merge_all(g - 2)
    merge_chip(n_groups - 1)
    merge_all(n_groups - 2)
    merge_all(n_groups - 1)
    for h in range(half_heads):
        ctx_ref[:, h * HEAD_DIM:(h + 1) * HEAD_DIM] = x_o[:, h, :].astype(BF16)

    def attn_copy(j):
        c = slice(j * BLK, (j + 1) * BLK)
        return pltpu.make_async_remote_copy(src_ref=part.at[0, :, c], dst_ref=arecv.at[:, c], send_sem=a_ss.at[j],
                                            recv_sem=a_rs.at[j], device_id=mate, device_id_type=MESH)

    for j in range(4):
        out_copy(j).wait()
        for n in range(2):
            c = slice((j % 2) * BLK + n * 256, (j % 2) * BLK + (n + 1) * 256)
            part[j // 2, :, c] = jnp.dot(ctx_ref[...], wbuf[4 + j // 2, (j % 2) * half_cols:(j % 2 + 1) * half_cols, n * 256:(n + 1) * 256],
                                         preferred_element_type=F32)
        if j < 2:
            attn_copy(j).start()
    for j in range(2):
        c = slice(j * BLK, (j + 1) * BLK)
        attn_copy(j).wait()
        y_ref[:, c] = part[1, :, c] + arecv[:, c]


def store_kernel(kv_ref, k_out, v_out, fresh, tiles, idx_v, idx_s, kvsem, tsem, isem):
    rows = k_out.shape[0]
    n_parts = kvsem.shape[1]
    per = rows // n_parts
    outs = (k_out, v_out)

    def big(a, p):
        r = pl.ds(p * per, per)
        return pltpu.make_async_copy(kv_ref.at[a, r], outs[a].at[r], kvsem.at[a, p])

    for a in range(2):
        for p in range(n_parts):
            big(a, p).start()

    idx_v[...] = kv_ref[0, rows, rows:rows + 32, :].astype(F32).astype(jnp.int32)
    idx_copy = pltpu.make_async_copy(idx_v, idx_s, isem)
    idx_copy.start()
    for a in range(2):
        fresh[a] = kv_ref[a, rows, 0:rows, :].astype(F32)
    idx_copy.wait()

    def tile_start(b):
        return pl.multiple_of(idx_s[0, b] * 16, 16)

    ids = lax.broadcasted_iota(jnp.int32, (16, HEAD_DIM), 0)

    def make_tile(b, _):
        hit = ids == idx_s[16, b]
        for a in range(2):
            old = kv_ref[a, b, pl.ds(tile_start(b), 16), :].astype(F32)
            tiles[a, b] = jnp.where(hit, fresh[a, pl.ds(b, 1), :], old).astype(BF16)
        return 0

    lax.fori_loop(0, rows, make_tile, 0, unroll=4)

    def small(a, b):
        return pltpu.make_async_copy(tiles.at[a, b], outs[a].at[b, pl.ds(tile_start(b), 16)], tsem.at[a, b])

    for a in range(2):
        for p in range(n_parts):
            big(a, p).wait()

            def put(b, _):
                small(a, b).start()
                return 0

            lax.fori_loop(p * per, (p + 1) * per, put, 0)
    for a in range(2):
        def done(b, _):
            small(a, b).wait()
            return 0

        lax.fori_loop(0, rows, done, 0)


ANY = pl.BlockSpec(memory_space=pl.ANY)
VM = pl.BlockSpec(memory_space=pltpu.VMEM)
SM = pl.BlockSpec(memory_space=pltpu.SMEM)
HB = pl.BlockSpec(memory_space=pltpu.HBM)


def device_step(hidden, ln_gamma, ln_beta, w_qkv, w_out, w_up, w_down, k_cache, v_cache, positions):
    rows, d_model = hidden.shape
    half_heads = w_out.shape[0] // HEAD_DIM // 2
    half_cols = half_heads * HEAD_DIM
    n_steps, n_groups = rows // STEP_ROWS, len(GROUPS)
    cos_full, sin_full = rope_tables(positions)
    dma = pltpu.SemaphoreType.DMA
    kv, mlp_chip, y = pl.pallas_call(
        layer_kernel,
        in_specs=[SM, VM, HB, VM, VM, VM, VM, HB, HB, HB, HB, HB, HB],
        out_specs=[VM] * 3,
        out_shape=[pltpu.VMEM((2, rows + 1) + k_cache.shape[1:], BF16),
                   jax.ShapeDtypeStruct((rows, half_cols), F32),
                   jax.ShapeDtypeStruct((rows, half_cols), F32)],
        scratch_shapes=[
            pltpu.VMEM((rows, d_model), BF16), pltpu.VMEM((rows, d_model), BF16),
            pltpu.VMEM((d_model, 2 * HEAD_DIM), BF16), pltpu.VMEM((6, d_model, BLK), BF16),
            pltpu.VMEM((2, rows, half_heads, HEAD_DIM), F32),
            pltpu.VMEM((rows, HEAD_DIM), F32), pltpu.VMEM((rows, HEAD_DIM), F32),
            pltpu.VMEM((rows, w_up.shape[1]), BF16), pltpu.VMEM((rows, half_cols), BF16),
            pltpu.VMEM((2, rows, half_cols), F32), pltpu.VMEM((rows, half_cols), F32), pltpu.VMEM((rows, half_cols), F32),
            pltpu.VMEM((2, rows, 3, half_heads, HEAD_DIM), F32),
            pltpu.VMEM((rows, 3, half_heads, HEAD_DIM), F32),
            pltpu.VMEM((rows, half_heads, HEAD_DIM), F32), pltpu.VMEM((n_groups, 2, half_heads, 128), F32),
            pltpu.VMEM((rows, half_heads, HEAD_DIM), F32), pltpu.VMEM((n_groups, 2, half_heads, 128), F32),
            dma, dma, dma((10,)), dma((4,)), dma((n_steps,)), dma((n_steps,)), dma, dma, dma, dma,
            dma((n_groups,)), dma((n_groups,)), dma((n_groups,)), dma((n_groups,)), dma((n_groups,)), dma((n_groups,)),
            dma((2,)), dma((2,)),
        ],
        compiler_params=pltpu.CompilerParams(collective_id=0, has_side_effects=True, vmem_limit_bytes=27 << 20),
    )(positions, positions.reshape(1, -1), hidden, ln_gamma.reshape(1, -1), ln_beta.reshape(1, -1), cos_full, sin_full,
      w_qkv, w_up, w_down, w_out, k_cache, v_cache)

    mlp_far = lax.ppermute(mlp_chip, 'sp', [(0, 2), (2, 0), (1, 3), (3, 1)])

    k_next, v_next = pl.pallas_call(
        store_kernel,
        in_specs=[VM],
        out_specs=[HB, HB],
        out_shape=[jax.ShapeDtypeStruct(k_cache.shape, BF16), jax.ShapeDtypeStruct(k_cache.shape, BF16)],
        scratch_shapes=[pltpu.VMEM((2, rows, HEAD_DIM), F32), pltpu.VMEM((2, rows, 16, HEAD_DIM), BF16),
                        pltpu.VMEM((32, rows), jnp.int32), pltpu.SMEM((32, rows), jnp.int32),
                        dma((2, 4)), dma((2, rows)), dma],
        compiler_params=pltpu.CompilerParams(vmem_limit_bytes=4 << 20),
        cost_estimate=pl.CostEstimate(flops=40_000_000_000, bytes_accessed=32 << 20, transcendentals=0),
    )(kv)

    half = y + (mlp_chip + mlp_far)
    mate_half = lax.ppermute(half, 'sp', [(0, 1), (1, 0), (2, 3), (3, 2)])
    first = (lax.axis_index('sp') % 2) == 0
    branches = jnp.concatenate([jnp.where(first, half, mate_half), jnp.where(first, mate_half, half)], axis=-1)
    out_hidden = (hidden.astype(F32) + branches).astype(BF16)
    return out_hidden, k_next, v_next


def solution(mesh):
    cache_spec = P('dp', 'sp', None)
    in_specs = (P('dp', None), P(None), P(None), P(None, None), P(None, None), P(None, 'sp'), P('sp', None), cache_spec, cache_spec, P('dp'))
    out_specs = (P('dp', None), cache_spec, cache_spec)
    return jax.shard_map(device_step, mesh=mesh, in_specs=in_specs, out_specs=out_specs, check_vma=False)
```

time: 153 us -> 81.3 us (0.53)
  Pallas kernels: 0 us -> 61.9 us
  matrix products: 42.2 us -> 0 us
  other arithmetic: 40.8 us -> 4.04 us
  waiting for transfers between devices: 43.2 us -> 13.5 us
  between operations: 14.2 us -> 0.71 us
  local copies, waits for them, and re-layouts: 12.1 us -> 0.01 us
    pallas_call x0 -> x2, Pallas kernels: none -> 61.9 us  [the longest x1 46.7 us: device_step(): pl.pallas_call(layer_kernel, in_specs=[SM, VM, HB, VM, VM, VM, VM, HB, HB...]
    dot_general x5 -> x0, matrix products: 42.2 us -> none  [the longest x1 12.2 us: local_stats(): jnp.einsum('bhd,bsd->bhs', q_rot, k_block, preferred_element_type=jnp.flo...]
    all_gather x1 -> x0, waiting for transfers between devices: 23.5 us -> none  [device_step(): all_stats = lax.all_gather(block_stats, 'sp')]
    select_n x1, other arithmetic: 23.3 us -> 0.11 us  [device_step(): jnp.where(first, half, mate_half)]
    psum x1 -> x0, waiting for transfers between devices: 19.7 us -> none  [device_step(): mlp_out = lax.psum(mlp_part, 'sp')]
    ppermute x0 -> x2, waiting for transfers between devices: none -> 13.5 us  [the longest x1 13.5 us: device_step(): mlp_far = lax.ppermute(mlp_chip, 'sp', [(0, 2), (2, 0), (1, 3), (3, 1)])]
    reduce_sum x5 -> x0, other arithmetic: 12.1 us -> none  [the longest x1 5.24 us: combine_stats(): total_ctx = jnp.sum(all_stats[..., :head_dim] * scale_w[..., None], axis=0)]
    all_gather x1 -> x0, local copies, waits for them, and re-layouts: 5.56 us -> none  [device_step(): all_stats = lax.all_gather(block_stats, 'sp')]
  transfers between devices with their start and end apart: 2 -> 2, of which waited for: 2 -> 1; matrix products, arithmetic and copies ran while one was open for 16% -> 0% of each run, Pallas kernels for 0% -> 19%
where the time goes in v1:
time: 81.3 us; the launch traced here: 81.1 us
  Pallas kernels  61.9 us (76%)
  waiting for transfers between devices  13.5 us (17%)
  other arithmetic  4.04 us (5%)
  starting transfers between devices  0.95 us (1%)
    pallas_call x1, Pallas kernels, device_step(): pl.pallas_call(layer_kernel, in_specs=[SM, VM, HB, VM, VM, VM, VM, HB, HB...  46.7 us
    pallas_call x1, Pallas kernels, device_step(): pl.pallas_call(store_kernel, in_specs=[VM], out_specs=[HB, HB], out_shape...  15.2 us
    ppermute x1, waiting for transfers between devices, device_step(): mlp_far = lax.ppermute(mlp_chip, 'sp', [(0, 2), (2, 0), (1, 3), (3, 1)])  13.5 us
  transfers between devices with their start and end apart: 2, of which 1 were waited for; matrix products, arithmetic and copies ran while one was open for 0% of the time, Pallas kernels for 19%

profile of v1, /device:TPU:0, one launch (start us, length us, event | category | flops | bytes accessed | tf_op | source)
XLA Modules:
  0.0 81.1 jit_solution(1785781013206611103)
XLA Ops:
  0.6 0.7 convert_element_type.10
  1.3 0.3 fusion.1
  1.6 0.8 pad_maximum_fusion
  2.4 46.7 %shard_map.121 = (bf16[2,129,512,128]{3,2,1,0:T(8,128)(2,1)S(1)}, f32[128,1024]{1,0:T(8,128)}, f32[128,1024]{1,0:T(8,128)}) custom-call(s32[128]{0:T(128)} %pos_ref.1, s32[1,128]{1,0:T(1,128)} %bitcast.5, bf16[128,2048]{1,0:T(8,128)(2,1)} %x_hbm.1, f32[1,2048]{1,0:T(1,128)} %bitcast.3, f32[1,2048]{1,0:T(1,128)} %bitcast.4, ...), custom_call_target="tpu_custom_call" | custom-call | tf_op jit(solution)/shard_map/pallas_call | solution.py:380
  49.1 0.9 %collective-permute-start = (f32[128,1024]{1,0:T(8,128)}, f32[128,1024]{1,0:T(8,128)S(1)}, u32[]{:S(2)}, u32[]{:S(2)}) collective-permute-start(f32[128,1024]{1,0:T(8,128)} %get-tuple-element.9), channel_id=1, source_target_pairs={{0,2},{2,0},{1,3},{3,1},{4,6},{6,4},{5,7},{7,5}} | collective-permute-start | bytes 1572872 | tf_op jit(solution)/shard_map/ppermute | solution.py:406
  50.0 13.5 %collective-permute-done = f32[128,1024]{1,0:T(8,128)S(1)} collective-permute-done((f32[128,1024]{1,0:T(8,128)}, f32[128,1024]{1,0:T(8,128)S(1)}, u32[]{:S(2)}, u32[]{:S(2)}) %collective-permute-start) | collective-permute-done | bytes 524320 | tf_op jit(solution)/shard_map/ppermute | solution.py:406
  63.5 1.3 %add_add_fusion = f32[128,1024]{1,0:T(8,128)S(1)} fusion(f32[128,1024]{1,0:T(8,128)} %get-tuple-element.8, f32[128,1024]{1,0:T(8,128)} %get-tuple-element.9, f32[128,1024]{1,0:T(8,128)S(1)} %collective-permute-done), kind=kLoop, calls=%fused_computation.2 | loop fusion | flops 262144 | bytes 2097152 | tf_op jit(solution)/shard_map/add | solution.py:420
  64.8 0.0 collective-permute-start.1
  64.8 0.0 copy-start
  64.9 15.2 %shard_map.122 = (bf16[128,512,128]{2,1,0:T(8,128)(2,1)}, bf16[128,512,128]{2,1,0:T(8,128)(2,1)}) custom-call(bf16[2,129,512,128]{3,2,1,0:T(8,128)(2,1)S(1)} %get-tuple-element.10.kv_ref), custom_call_target="tpu_custom_call" | custom-call | flops 40000000000 | bytes 33554432 | tf_op jit(solution)/shard_map/pallas_call | solution.py:408
  80.1 0.0 collective-permute-done.1
  80.1 0.1 broadcast_select_fusion.1
  80.2 0.0 copy-done
  80.2 0.9 %fusion = bf16[128,2048]{1,0:T(8,128)(2,1)} fusion(f32[128,1024]{1,0:T(8,128)S(1)} %get-tuple-element.14, f32[128,1024]{1,0:T(8,128)S(1)} %get-tuple-element.13, bf16[128,2048]{1,0:T(8,128)(2,1)S(1)} %copy-done), kind=kLoop, calls=%fused_computation.1 | loop fusion | flops 1048576 | bytes 2097152 | tf_op jit(solution)/shard_map/convert_element_type | solution.py:424
  (1 shorter events, 0.0 us)
Async XLA Ops:
  49.1 14.4 %collective-permute-start = (f32[128,1024]{1,0:T(8,128)}, f32[128,1024]{1,0:T(8,128)S(1)}, u32[]{:S(2)}, u32[]{:S(2)}) collective-permute-start(f32[128,1024]{1,0:T(8,128)} %get-tuple-element.9), channel_id=1, source_target_pairs={{0,2},{2,0},{1,3},{3,1},{4,6},{6,4},{5,7},{7,5}} | collective-permute-start | bytes 1572872 | tf_op jit(solution)/shard_map/ppermute | solution.py:406
  64.8 15.3 %collective-permute-start.1 = (f32[128,1024]{1,0:T(8,128)S(1)}, f32[128,1024]{1,0:T(8,128)S(1)}, u32[]{:S(2)}, u32[]{:S(2)}) collective-permute-start(f32[128,1024]{1,0:T(8,128)S(1)} %add_add_fusion), channel_id=1, source_target_pairs={{0,1},{1,0},{2,3},{3,2},{4,5},{5,4},{6,7},{7,6}} | collective-permute-start | bytes 1572872 | tf_op jit(solution)/shard_map/ppermute | solution.py:421
  64.8 15.4 %copy-start = (bf16[128,2048]{1,0:T(8,128)(2,1)S(1)}, bf16[128,2048]{1,0:T(8,128)(2,1)}, u32[]{:S(2)}) copy-start(bf16[128,2048]{1,0:T(8,128)(2,1)} %x_hbm.1) | copy-start | bytes 1572868

commit v2 on v1

v2 whole, which is shorter than its diff:
```python
import jax
import jax.numpy as jnp
import numpy as np
from jax import lax
from jax.experimental import pallas as pl
from jax.experimental.pallas import tpu as pltpu
from jax.sharding import PartitionSpec as P


MESH = pl.DeviceIdType.MESH
LN_EPS = 1e-5
ROPE_BASE = 10000.0
NEG_FILL = -1e30
HEAD_DIM = 128
BLK = 512
STEP_ROWS = 8
SLOTS = 7
FAR_GROUPS = (32, 32)
OWN_GROUPS = (32, 24, 8)
F32, BF16 = jnp.float32, jnp.bfloat16


def rope_tables(positions):
    inv_freq = (ROPE_BASE ** (-np.arange(0, HEAD_DIM, 2) / HEAD_DIM)).astype(np.float32)
    angles = positions.astype(F32)[:, None] * inv_freq[None, :]
    cos_half, sin_half = jnp.cos(angles), jnp.sin(angles)
    return jnp.concatenate([cos_half, cos_half], axis=-1), jnp.concatenate([-sin_half, sin_half], axis=-1)


def layer_kernel(pos_hbm, posv_hbm, x_hbm, gamma_hbm, beta_hbm, cos_hbm, sin_hbm, wqkv_hbm, wup_hbm, wdown_hbm, wout_hbm,
                 k_hbm, v_hbm, kv_ref, z_ref,
                 pos_ref, posv_ref, gamma_ref, beta_ref, cos_ref, sin_ref,
                 xbuf, hbuf, kvw, wbuf, q_s, kn_ref, vn_ref, act, ctx_ref, part, mrecv, mx_recv, mlp_own, mlp_mate, arecv,
                 s_loc, s_recv, chip_o, chip_ml, x_o, x_ml,
                 insem, xsem, kvwsem, wsem, osem, ksem, vsem, q_ss, q_rs, m_ss, m_rs, mx_ss, mx_rs, mm_ss, mm_rs,
                 c_ss, c_rs, o_ss, o_rs, t_ss, t_rs, a_ss, a_rs):
    dp, sp = lax.axis_index('dp'), lax.axis_index('sp')
    core = lax.rem(sp, 2)
    chip = lax.div(sp, 2)
    mate = (dp, sp + 1 - 2 * core)
    across = (dp, lax.rem(sp + 2, 4))
    rows = xbuf.shape[0]
    own_rows = rows // 2
    n_steps = rows // STEP_ROWS
    seq_dev = k_hbm.shape[1]
    half_heads = q_s.shape[2]
    half_cols = half_heads * HEAD_DIM
    scale = HEAD_DIM ** -0.5
    own_base = pl.multiple_of(chip * own_rows, own_rows)
    far_base = pl.multiple_of((1 - chip) * own_rows, own_rows)

    def weight_copy(src, col, slot, idx):
        return pltpu.make_async_copy(src.at[:, pl.ds(pl.multiple_of(col, BLK), BLK)], wbuf.at[slot], wsem.at[idx])

    def q_copy(j):
        return weight_copy(wqkv_hbm, core * half_cols + j * BLK, j, j)

    def up_copy(j):
        return weight_copy(wup_hbm, j * BLK, 2 + j, 2 + j)

    def down_copy(j):
        half = jnp.where(j < 2, 1 - core, core)
        return weight_copy(wdown_hbm, half * half_cols + lax.rem(j, 2) * BLK, lax.rem(6 + j, SLOTS), 6 + j)

    def out_copy(j):
        half = (1 - core) if j < 2 else core
        src = wout_hbm.at[pl.ds(pl.multiple_of(core * half_cols, half_cols), half_cols),
                          pl.ds(pl.multiple_of(half * half_cols + (j % 2) * BLK, BLK), BLK)]
        return pltpu.make_async_copy(src, wbuf.at[3 + j // 2, pl.ds((j % 2) * half_cols, half_cols)], osem.at[j])

    def first_row(i):
        return pl.multiple_of(lax.rem((1 - chip) * own_rows + i * STEP_ROWS, rows), STEP_ROWS)

    def k_copy(i):
        r = pl.ds(first_row(i), STEP_ROWS)
        return pltpu.make_async_copy(k_hbm.at[r], kv_ref.at[0, r], ksem.at[i])

    def v_copy(i):
        r = pl.ds(first_row(i), STEP_ROWS)
        return pltpu.make_async_copy(v_hbm.at[r], kv_ref.at[1, r], vsem.at[i])

    def cache_start(i):
        k_copy(i).start()
        v_copy(i).start()

    x_copy = pltpu.make_async_copy(x_hbm, xbuf, xsem)
    x_copy.start()
    small = [pltpu.make_async_copy(src, dst, insem.at[n]) for n, (src, dst) in enumerate((
        (gamma_hbm, gamma_ref), (beta_hbm, beta_ref), (cos_hbm, cos_ref), (sin_hbm, sin_ref), (posv_hbm, posv_ref),
        (pos_hbm, pos_ref)))]
    for copy in small:
        copy.start()
    kvw_copy = pltpu.make_async_copy(wqkv_hbm.at[:, pl.ds(2 * half_cols, 2 * HEAD_DIM)], kvw, kvwsem)
    kvw_copy.start()
    for j in range(2):
        q_copy(j).start()
    for j in range(4):
        up_copy(j).start()
    down_copy(0).start()

    barrier = pltpu.get_barrier_semaphore()
    for dev in (mate, across):
        pl.semaphore_signal(barrier, inc=1, device_id=dev, device_id_type=MESH)
    pl.semaphore_wait(barrier, 2)

    x_copy.wait()
    for copy in small:
        copy.wait()

    def norm_rows(i, _):
        for u in range(2):
            r = pl.ds(pl.multiple_of(i * 32 + u * 16, 16), 16)
            h = xbuf[r, :].astype(F32)
            centered = h - jnp.mean(h, axis=-1, keepdims=True)
            var = jnp.mean(centered * centered, axis=-1, keepdims=True)
            hbuf[r, :] = (centered * lax.rsqrt(var + LN_EPS) * gamma_ref[...] + beta_ref[...]).astype(BF16)
        return 0

    lax.fori_loop(0, rows // 32, norm_rows, 0)

    def rotate(vec):
        vec = vec.astype(BF16).astype(F32)
        return (vec * cos_ref[...] + pltpu.roll(vec, HEAD_DIM // 2, 1) * sin_ref[...]).astype(BF16)

    kvw_copy.wait()
    kv_new = jnp.dot(hbuf[...], kvw[...], preferred_element_type=F32)
    k_new = rotate(kv_new[:, :HEAD_DIM])
    v_new = kv_new[:, HEAD_DIM:].astype(BF16)
    kn_ref[...] = k_new.astype(F32)
    vn_ref[...] = v_new.astype(F32)
    kv_ref[0, rows, 0:rows, :] = k_new
    kv_ref[1, rows, 0:rows, :] = v_new
    at = jnp.broadcast_to(posv_ref[...] - sp * seq_dev, (16, rows))
    tile = lax.shift_right_logical(jnp.clip(at, 0, seq_dev - 1), 4)
    inside = jnp.logical_and(at >= 0, at < seq_dev)
    kv_ref[0, rows, rows:rows + 16, :] = tile.astype(F32).astype(BF16)
    kv_ref[0, rows, rows + 16:rows + 32, :] = jnp.where(inside, at - tile * 16, 16).astype(F32).astype(BF16)

    for j in range(2):
        q_copy(j).wait()
        for n in range(2):
            q_part = jnp.dot(hbuf[...], wbuf[j, :, n * 256:(n + 1) * 256], preferred_element_type=F32)
            for t in range(2):
                q_s[core, :, j * 4 + n * 2 + t, :] = rotate(q_part[:, t * HEAD_DIM:(t + 1) * HEAD_DIM]).astype(F32)
        down_copy(1 + j).start()
    q_send = pltpu.make_async_remote_copy(src_ref=q_s.at[core], dst_ref=q_s.at[core], send_sem=q_ss, recv_sem=q_rs,
                                          device_id=mate, device_id_type=MESH)
    q_send.start()

    def up_step(j, _):
        up_copy(j).wait()
        for n in range(2):
            up = jnp.dot(hbuf[...], wbuf[2 + j, :, n * 256:(n + 1) * 256], preferred_element_type=F32)
            gelu = 0.5 * up * (1.0 + lax.erf(up * (0.5 ** 0.5)))
            act[:, pl.ds(pl.multiple_of(j * BLK + n * 256, 256), 256)] = gelu.astype(BF16)

        @pl.when(j == 0)
        def _():
            down_copy(3).start()
            cache_start(0)

        @pl.when(j > 0)
        def _():
            cache_start(2 * j - 1)
            cache_start(2 * j)

        return 0

    lax.fori_loop(0, 4, up_step, 0)

    def down_step(j, _):
        down_copy(j).wait()
        slot = lax.rem(6 + j, SLOTS)
        for n in range(2):
            part[j // 2, :, pl.ds(pl.multiple_of(lax.rem(j, 2) * BLK + n * 256, 256), 256)] = jnp.dot(
                act[...], wbuf[slot, :, n * 256:(n + 1) * 256], preferred_element_type=F32)
        cache_start(7 + 2 * j)
        cache_start(8 + 2 * j)
        return 0

    m_send = pltpu.make_async_remote_copy(src_ref=part.at[0], dst_ref=mrecv, send_sem=m_ss, recv_sem=m_rs,
                                          device_id=mate, device_id_type=MESH)
    lax.fori_loop(0, 2, down_step, 0)
    m_send.start()
    lax.fori_loop(2, 4, down_step, 0)
    cache_start(n_steps - 1)
    for j in range(4):
        out_copy(j).start()
    m_send.wait()
    part[1] = part[1] + mrecv[...]
    mx_send = pltpu.make_async_remote_copy(src_ref=part.at[1, pl.ds(far_base, own_rows)], dst_ref=mx_recv, send_sem=mx_ss,
                                           recv_sem=mx_rs, device_id=across, device_id_type=MESH)
    mx_send.start()
    q_send.wait()

    slots = lax.broadcasted_iota(jnp.int32, (2 * half_heads, seq_dev), 1)
    lanes = lax.broadcasted_iota(jnp.int32, (half_heads, 128), 1)
    zero_q = jnp.zeros((2 * half_heads, HEAD_DIM), BF16)

    def attend(i, _):
        k_copy(i).wait()
        v_copy(i).wait()
        row = first_row(i)
        for pair in range(STEP_ROWS // 2):
            bs = [row + 2 * pair + t for t in range(2)]
            qf = [jnp.concatenate([q_s[0, b], q_s[1, b]], axis=0) for b in bs]
            qb = [q.astype(BF16) for q in qf]
            lhs = jnp.concatenate([jnp.concatenate([qb[0], zero_q], axis=1), jnp.concatenate([zero_q, qb[1]], axis=1)], axis=0)
            k2 = jnp.concatenate([kv_ref[0, b] for b in bs], axis=1)
            s2 = lax.dot_general(lhs, k2, (((1,), (1,)), ((), ())), preferred_element_type=F32) * scale
            probs, stats = [], []
            for t, b in enumerate(bs):
                at = pos_ref[b] - sp * seq_dev
                s = s2[t * 2 * half_heads:(t + 1) * 2 * half_heads]
                old = slots < at
                here = jnp.logical_and(at >= 0, at < seq_dev)
                masked = jnp.where(old, s, NEG_FILL)
                s_new = jnp.sum(qf[t] * kn_ref[pl.ds(b, 1), :], axis=-1, keepdims=True) * scale
                s_new = jnp.where(here, s_new, NEG_FILL)
                m = jnp.maximum(jnp.max(masked, axis=-1, keepdims=True), s_new)
                e = jnp.where(old, jnp.exp(masked - m), 0.0)
                e_new = jnp.where(here, jnp.exp(s_new - m), 0.0)
                l = jnp.sum(e, axis=-1, keepdims=True) + e_new
                probs.append(e.astype(BF16))
                stats.append((m, l, e_new.astype(BF16).astype(F32) * vn_ref[pl.ds(b, 1), :]))
            v2 = jnp.concatenate([kv_ref[1, b] for b in bs], axis=1)
            o2 = jnp.dot(jnp.concatenate(probs, axis=0), v2, preferred_element_type=F32)
            for t in range(2):
                m, l, extra = stats[t]
                o = o2[t * 2 * half_heads:(t + 1) * 2 * half_heads, t * HEAD_DIM:(t + 1) * HEAD_DIM] + extra
                mb = jnp.broadcast_to(m, o.shape)
                lb = jnp.broadcast_to(l, o.shape)
                turn = i * STEP_ROWS + 2 * pair + t
                for f in range(2):
                    hs = slice(f * half_heads, (f + 1) * half_heads)
                    s_loc[f, turn, 0] = o[hs]
                    s_loc[f, turn, 1] = mb[hs]
                    s_loc[f, turn, 2] = lb[hs]
        return 0

    sizes = FAR_GROUPS + OWN_GROUPS
    starts = [sum(sizes[:g]) for g in range(len(sizes))]
    n_far = len(FAR_GROUPS)

    def swap_copy(g):
        r = pl.ds(starts[g], sizes[g])
        return pltpu.make_async_remote_copy(src_ref=s_loc.at[1 - core, r], dst_ref=s_recv.at[r], send_sem=c_ss.at[g],
                                            recv_sem=c_rs.at[g], device_id=mate, device_id_type=MESH)

    def cross_copies(g):
        r = pl.ds(starts[g], sizes[g])
        return (pltpu.make_async_remote_copy(src_ref=chip_o.at[r], dst_ref=x_o.at[r], send_sem=o_ss.at[g],
                                             recv_sem=o_rs.at[g], device_id=across, device_id_type=MESH),
                pltpu.make_async_remote_copy(src_ref=chip_ml.at[g], dst_ref=x_ml.at[g], send_sem=t_ss.at[g],
                                             recv_sem=t_rs.at[g], device_id=across, device_id_type=MESH))

    def merge_far(g):
        swap_copy(g).wait()

        def body(i, tiles):
            tm, tl = tiles
            for u in range(8):
                b = starts[g] + i * 8 + u
                m_a, m_b = s_loc[core, b, 1], s_recv[b, 1]
                top = jnp.maximum(m_a, m_b)
                w_a, w_b = jnp.exp(m_a - top), jnp.exp(m_b - top)
                chip_o[b] = s_loc[core, b, 0] * w_a + s_recv[b, 0] * w_b
                total = s_loc[core, b, 2] * w_a + s_recv[b, 2] * w_b
                hit = lanes == i * 8 + u
                tm = jnp.where(hit, top, tm)
                tl = jnp.where(hit, total, tl)
            return tm, tl

        zero = jnp.zeros((half_heads, 128), F32)
        tm, tl = lax.fori_loop(0, sizes[g] // 8, body, (zero, zero))
        chip_ml[g, 0] = tm
        chip_ml[g, 1] = tl
        for copy in cross_copies(g):
            copy.start()

    def merge_own(g):
        swap_copy(g).wait()

        def body(i, _):
            for u in range(8):
                b = starts[g] + i * 8 + u
                src = b - own_rows
                part_g = starts[g] - own_rows
                xg = [n for n in range(n_far) if starts[n] <= part_g][-1]
                hit = lanes == src - starts[xg]
                m_x = jnp.sum(jnp.where(hit, x_ml[xg, 0], 0.0), axis=-1, keepdims=True)
                l_x = jnp.sum(jnp.where(hit, x_ml[xg, 1], 0.0), axis=-1, keepdims=True)
                m_a, m_b = s_loc[core, b, 1], s_recv[b, 1]
                top = jnp.maximum(jnp.maximum(m_a, m_b), m_x)
                w_a, w_b, w_x = jnp.exp(m_a - top), jnp.exp(m_b - top), jnp.exp(m_x - top)
                total = s_loc[core, b, 2] * w_a + s_recv[b, 2] * w_b + l_x * w_x
                x_o[src] = (s_loc[core, b, 0] * w_a + s_recv[b, 0] * w_b + x_o[src] * w_x) / total
            return 0

        lax.fori_loop(0, sizes[g] // 8, body, 0)

    def run_group(g):
        lax.fori_loop(starts[g] // STEP_ROWS, (starts[g] + sizes[g]) // STEP_ROWS, attend, 0)
        swap_copy(g).start()

    def cross_wait(g):
        for copy in cross_copies(g):
            copy.wait()

    mm_send = pltpu.make_async_remote_copy(src_ref=mlp_own, dst_ref=mlp_mate, send_sem=mm_ss, recv_sem=mm_rs,
                                           device_id=mate, device_id_type=MESH)
    run_group(0)
    run_group(1)
    merge_far(0)
    run_group(2)
    merge_far(1)
    run_group(3)
    mx_send.wait()
    mlp_own[...] = part[1, pl.ds(own_base, own_rows), :] + mx_recv[...]
    mm_send.start()
    run_group(4)
    cross_wait(0)
    merge_own(2)
    cross_wait(1)
    merge_own(3)
    merge_own(4)
    for h in range(half_heads):
        ctx_ref[:, h * HEAD_DIM:(h + 1) * HEAD_DIM] = x_o[:, h, :].astype(BF16)
    mm_send.wait()

    def attn_copy(j):
        return pltpu.make_async_remote_copy(src_ref=part.at[0, pl.ds(j % 2 * own_rows, own_rows), pl.ds(j // 2 * BLK, BLK)],
                                            dst_ref=arecv.at[j], send_sem=a_ss.at[j], recv_sem=a_rs.at[j],
                                            device_id=mate, device_id_type=MESH)

    def block(j):
        return part.at[0, pl.ds(j % 2 * own_rows, own_rows), pl.ds(j // 2 * BLK, BLK)]

    for j in range(4):
        out_copy(j).wait()
        for n in range(2):
            block(j)[:, n * 256:(n + 1) * 256] = jnp.dot(
                ctx_ref[...], wbuf[3 + j // 2, (j % 2) * half_cols:(j % 2 + 1) * half_cols, n * 256:(n + 1) * 256],
                preferred_element_type=F32)
        attn_copy(j).start()
    for j in range(4):
        attn_copy(j).wait()
    for j in range(4):
        half = (1 - core) if j < 2 else core
        mlp = mlp_mate if j < 2 else mlp_own
        col = pl.multiple_of(half * half_cols + (j % 2) * BLK, BLK)
        z_ref[:, pl.ds(col, BLK)] = block(j)[...] + arecv[(j + 2) % 4] + mlp[:, (j % 2) * BLK:(j % 2 + 1) * BLK]


def store_kernel(kv_ref, k_out, v_out, fresh, tiles, idx_v, idx_s, kvsem, tsem, isem):
    rows = k_out.shape[0]
    n_parts = kvsem.shape[1]
    per = rows // n_parts
    outs = (k_out, v_out)

    def big(a, p):
        r = pl.ds(p * per, per)
        return pltpu.make_async_copy(kv_ref.at[a, r], outs[a].at[r], kvsem.at[a, p])

    idx_v[...] = kv_ref[0, rows, rows:rows + 32, :].astype(F32).astype(jnp.int32)
    idx_copy = pltpu.make_async_copy(idx_v, idx_s, isem)
    idx_copy.start()
    for p in range(n_parts):
        for a in range(2):
            big(a, p).start()
    for a in range(2):
        fresh[a] = kv_ref[a, rows, 0:rows, :].astype(F32)
    idx_copy.wait()
    ids = lax.broadcasted_iota(jnp.int32, (16, HEAD_DIM), 0)

    def tile_of(b):
        return pl.ds(pl.multiple_of(idx_s[0, b] * 16, 16), 16)

    def make_tile(b, _):
        hit = ids == idx_s[16, b]
        for a in range(2):
            old = kv_ref[a, b, tile_of(b), :].astype(F32)
            tiles[a, b] = jnp.where(hit, fresh[a, pl.ds(b, 1), :], old).astype(BF16)
        return 0

    lax.fori_loop(0, rows, make_tile, 0, unroll=8)

    for p in range(n_parts):
        for a in range(2):
            big(a, p).wait()

        def put(b, _):
            for a in range(2):
                pltpu.make_async_copy(tiles.at[a, b], outs[a].at[b, tile_of(b)], tsem.at[a]).start()
            return 0

        lax.fori_loop(p * per, (p + 1) * per, put, 0, unroll=4)
    for a in range(2):
        pltpu.make_async_copy(tiles.at[a], outs[a].at[:, pl.ds(0, 16)], tsem.at[a]).wait()


ANY = pl.BlockSpec(memory_space=pl.ANY)
VM = pl.BlockSpec(memory_space=pltpu.VMEM)
SM = pl.BlockSpec(memory_space=pltpu.SMEM)
HB = pl.BlockSpec(memory_space=pltpu.HBM)


def device_step(hidden, ln_gamma, ln_beta, w_qkv, w_out, w_up, w_down, k_cache, v_cache, positions):
    rows, d_model = hidden.shape
    half_heads = w_out.shape[0] // HEAD_DIM // 2
    half_cols = half_heads * HEAD_DIM
    own_rows = rows // 2
    n_steps, n_far, n_all = rows // STEP_ROWS, len(FAR_GROUPS), len(FAR_GROUPS) + len(OWN_GROUPS)
    positions, upper = lax.optimization_barrier((positions, lax.axis_index('sp') < 2))
    cos_full, sin_full = rope_tables(positions)
    dma = pltpu.SemaphoreType.DMA
    heads_f32 = (half_heads, HEAD_DIM)
    kv, z = pl.pallas_call(
        layer_kernel,
        in_specs=[HB] * 13,
        out_specs=[VM] * 2,
        out_shape=[pltpu.VMEM((2, rows + 1) + k_cache.shape[1:], BF16), jax.ShapeDtypeStruct((own_rows, d_model), F32)],
        scratch_shapes=[
            pltpu.SMEM((rows,), jnp.int32), pltpu.VMEM((1, rows), jnp.int32),
            pltpu.VMEM((1, d_model), F32), pltpu.VMEM((1, d_model), F32),
            pltpu.VMEM((rows, HEAD_DIM), F32), pltpu.VMEM((rows, HEAD_DIM), F32),
            pltpu.VMEM((rows, d_model), BF16), pltpu.VMEM((rows, d_model), BF16),
            pltpu.VMEM((d_model, 2 * HEAD_DIM), BF16), pltpu.VMEM((SLOTS, d_model, BLK), BF16),
            pltpu.VMEM((2, rows) + heads_f32, F32),
            pltpu.VMEM((rows, HEAD_DIM), F32), pltpu.VMEM((rows, HEAD_DIM), F32),
            pltpu.VMEM((rows, w_up.shape[1]), BF16), pltpu.VMEM((own_rows, half_cols), BF16),
            pltpu.VMEM((2, rows, half_cols), F32), pltpu.VMEM((rows, half_cols), F32),
            pltpu.VMEM((own_rows, half_cols), F32), pltpu.VMEM((own_rows, half_cols), F32), pltpu.VMEM((own_rows, half_cols), F32),
            pltpu.VMEM((4, own_rows, BLK), F32),
            pltpu.VMEM((2, rows, 3) + heads_f32, F32), pltpu.VMEM((rows, 3) + heads_f32, F32),
            pltpu.VMEM((own_rows,) + heads_f32, F32), pltpu.VMEM((n_far, 2) + heads_f32, F32),
            pltpu.VMEM((own_rows,) + heads_f32, F32), pltpu.VMEM((n_far, 2) + heads_f32, F32),
            dma((6,)), dma, dma, dma((10,)), dma((4,)), dma((n_steps,)), dma((n_steps,)), dma, dma, dma, dma, dma, dma, dma, dma,
            dma((n_all,)), dma((n_all,)), dma((n_far,)), dma((n_far,)), dma((n_far,)), dma((n_far,)), dma((4,)), dma((4,)),
        ],
        compiler_params=pltpu.CompilerParams(collective_id=0, has_side_effects=True, vmem_limit_bytes=27 << 20),
    )(positions, positions.reshape(1, -1), hidden, ln_gamma.reshape(1, -1), ln_beta.reshape(1, -1), cos_full, sin_full,
      w_qkv, w_up, w_down, w_out, k_cache, v_cache)

    z_far = lax.ppermute(z, 'sp', [(0, 2), (2, 0), (1, 3), (3, 1)])

    k_next, v_next = pl.pallas_call(
        store_kernel,
        in_specs=[VM],
        out_specs=[HB, HB],
        out_shape=[jax.ShapeDtypeStruct(k_cache.shape, BF16), jax.ShapeDtypeStruct(k_cache.shape, BF16)],
        scratch_shapes=[pltpu.VMEM((2, rows, HEAD_DIM), F32), pltpu.VMEM((2, rows, 16, HEAD_DIM), BF16),
                        pltpu.VMEM((32, rows), jnp.int32), pltpu.SMEM((32, rows), jnp.int32),
                        dma((2, 8)), dma((2,)), dma],
        compiler_params=pltpu.CompilerParams(vmem_limit_bytes=4 << 20),
        cost_estimate=pl.CostEstimate(flops=40_000_000_000, bytes_accessed=32 << 20, transcendentals=0),
    )(kv)

    branches = jnp.concatenate([jnp.where(upper, z, z_far), jnp.where(upper, z_far, z)], axis=0)
    out_hidden = (hidden.astype(F32) + branches).astype(BF16)
    return out_hidden, k_next, v_next


def solution(mesh):
    cache_spec = P('dp', 'sp', None)
    in_specs = (P('dp', None), P(None), P(None), P(None, None), P(None, None), P(None, 'sp'), P('sp', None), cache_spec, cache_spec, P('dp'))
    out_specs = (P('dp', None), cache_spec, cache_spec)
    return jax.shard_map(device_step, mesh=mesh, in_specs=in_specs, out_specs=out_specs, check_vma=False)
```

time: 81.3 us -> 57.8 us (0.71)
  waiting for transfers between devices: 13.5 us -> 0.79 us
  Pallas kernels: 61.9 us -> 51.2 us
    ppermute x2 -> x1, waiting for transfers between devices: 13.5 us -> 0.79 us  [device_step(): z_far = lax.ppermute(z, 'sp', [(0, 2), (2, 0), (1, 3), (3, 1)])]
    pallas_call x1, Pallas kernels: 46.7 us -> 39.3 us  [device_step(): pl.pallas_call(layer_kernel, in_specs=[HB] * 13, out_specs=[VM] * 2, out_...]
    pallas_call x1, Pallas kernels: 15.2 us -> 11.9 us  [device_step(): pl.pallas_call(store_kernel, in_specs=[VM], out_specs=[HB, HB], out_shape...]
    add x1 -> x0, other arithmetic: 1.29 us -> none  [device_step(): half = y + (mlp_chip + mlp_far)]
    ppermute x2 -> x1, starting transfers between devices: 0.95 us -> 1.71 us  [device_step(): z_far = lax.ppermute(z, 'sp', [(0, 2), (2, 0), (1, 3), (3, 1)])]
  transfers between devices with their start and end apart: 2 -> 1, of which waited for: 1 -> 1; matrix products, arithmetic and copies ran while one was open for 0% -> 0% of each run, Pallas kernels for 19% -> 21%
where the time goes in v2:
time: 57.8 us; the launch traced here: 57.7 us
  Pallas kernels  51.2 us (89%)
  other arithmetic  3.36 us (6%)
  starting transfers between devices  1.71 us (3%)
  waiting for transfers between devices  0.79 us (1%)
  between operations  0.68 us (1%)
    pallas_call x1, Pallas kernels, device_step(): pl.pallas_call(layer_kernel, in_specs=[HB] * 13, out_specs=[VM] * 2, out_...  39.3 us
    pallas_call x1, Pallas kernels, device_step(): pl.pallas_call(store_kernel, in_specs=[VM], out_specs=[HB, HB], out_shape...  11.9 us
    ppermute x1, starting transfers between devices, device_step(): z_far = lax.ppermute(z, 'sp', [(0, 2), (2, 0), (1, 3), (3, 1)])  1.71 us
  transfers between devices with their start and end apart: 1, of which 1 were waited for; matrix products, arithmetic and copies ran while one was open for 0% of the time, Pallas kernels for 21%

profile of v2, /device:TPU:0, one launch (start us, length us, event | category | flops | bytes accessed | tf_op | source)
XLA Modules:
  0.0 57.7 jit_solution(2783977645128267511)
XLA Ops:
  0.6 0.7 %convert_element_type.10 = f32[128]{0:T(128)S(1)} convert(s32[128]{0:T(128)} %pos_hbm) | non-fusion elementwise | flops 128 | bytes 1024 | tf_op jit(solution)/shard_map/convert_element_type | solution.py:25
  1.3 1.0 %fusion.1 = (f32[128,64]{1,0:T(8,128)S(1)}, f32[128,64]{1,0:T(8,128)S(1)}, f32[128,64]{1,0:T(8,128)S(1)}) fusion(f32[64]{0:T(128)} %constant.9, f32[128]{0:T(128)S(1)} %convert_element_type.10), kind=kLoop, calls=%fused_computation.8 | loop fusion | flops 16384 | bytes 99072 | tf_op jit(solution)/shard_map/neg | solution.py:27
  2.3 0.8 %pad_maximum_fusion = (f32[128,128]{1,0:T(8,128)}, f32[128,128]{1,0:T(8,128)}) fusion(f32[128,64]{1,0:T(8,128)S(1)} %get-tuple-element.19, f32[128,64]{1,0:T(8,128)S(1)} %get-tuple-element.18, f32[128,64]{1,0:T(8,128)S(1)} %get-tuple-element.17), kind=kLoop, calls=%fused_computation.6 | loop fusion | flops 32768 | bytes 229376 | tf_op jit(solution)/shard_map/concatenate | solution.py:27
  3.0 39.3 %shard_map.130 = (bf16[2,129,512,128]{3,2,1,0:T(8,128)(2,1)S(1)}, f32[64,2048]{1,0:T(8,128)}) custom-call(s32[128]{0:T(128)} %pos_hbm, s32[1,128]{1,0:T(1,128)} %bitcast.5, bf16[128,2048]{1,0:T(8,128)(2,1)} %x_hbm.1, f32[1,2048]{1,0:T(1,128)} %bitcast.3, f32[1,2048]{1,0:T(1,128)} %bitcast.4, f32[128,128]{1,0:T(8,128)} %get-tuple-element.20.cos_hbm, ...), custom_call_target="tpu_custom_call" | custom-call | tf_op jit(solution)/shard_map/pallas_call | solution.py:418
  42.3 1.7 %collective-permute-start = (f32[64,2048]{1,0:T(8,128)}, f32[64,2048]{1,0:T(8,128)S(1)}, u32[]{:S(2)}, u32[]{:S(2)}) collective-permute-start(f32[64,2048]{1,0:T(8,128)} %get-tuple-element.11), channel_id=1, source_target_pairs={{0,2},{2,0},{1,3},{3,1},{4,6},{6,4},{5,7},{7,5}} | collective-permute-start | bytes 1572872 | tf_op jit(solution)/shard_map/ppermute | solution.py:445
  44.0 0.0 copy-start.1
  44.0 0.0 copy-start
  44.0 11.9 %shard_map.131 = (bf16[128,512,128]{2,1,0:T(8,128)(2,1)}, bf16[128,512,128]{2,1,0:T(8,128)(2,1)}) custom-call(bf16[2,129,512,128]{3,2,1,0:T(8,128)(2,1)S(1)} %get-tuple-element.12.kv_ref), custom_call_target="tpu_custom_call" | custom-call | flops 40000000000 | bytes 33554432 | tf_op jit(solution)/shard_map/pallas_call | solution.py:447
  55.9 0.8 %collective-permute-done = f32[64,2048]{1,0:T(8,128)S(1)} collective-permute-done((f32[64,2048]{1,0:T(8,128)}, f32[64,2048]{1,0:T(8,128)S(1)}, u32[]{:S(2)}, u32[]{:S(2)}) %collective-permute-start) | collective-permute-done | bytes 524320 | tf_op jit(solution)/shard_map/ppermute | solution.py:445
  56.7 0.0 copy-done.1
  56.7 0.1 broadcast_select_fusion.1
  56.8 0.0 copy-done
  56.8 0.9 %fusion = bf16[128,2048]{1,0:T(8,128)(2,1)} fusion(f32[64,2048]{1,0:T(8,128)S(1)} %get-tuple-element.16, f32[64,2048]{1,0:T(8,128)S(1)} %get-tuple-element.15, bf16[128,2048]{1,0:T(8,128)(2,1)S(1)} %copy-done), kind=kLoop, calls=%fused_computation.1 | loop fusion | flops 1048576 | bytes 2097152 | tf_op jit(solution)/shard_map/convert_element_type | solution.py:460
Async XLA Ops:
  42.3 14.4 %collective-permute-start = (f32[64,2048]{1,0:T(8,128)}, f32[64,2048]{1,0:T(8,128)S(1)}, u32[]{:S(2)}, u32[]{:S(2)}) collective-permute-start(f32[64,2048]{1,0:T(8,128)} %get-tuple-element.11), channel_id=1, source_target_pairs={{0,2},{2,0},{1,3},{3,1},{4,6},{6,4},{5,7},{7,5}} | collective-permute-start | bytes 1572872 | tf_op jit(solution)/shard_map/ppermute | solution.py:445
  44.0 12.7 %copy-start.1 = (f32[64,2048]{1,0:T(8,128)S(1)}, f32[64,2048]{1,0:T(8,128)}, u32[]{:S(2)}) copy-start(f32[64,2048]{1,0:T(8,128)} %get-tuple-element.11) | copy-start | bytes 1572868
  44.0 12.8 %copy-start = (bf16[128,2048]{1,0:T(8,128)(2,1)S(1)}, bf16[128,2048]{1,0:T(8,128)(2,1)}, u32[]{:S(2)}) copy-start(bf16[128,2048]{1,0:T(8,128)(2,1)} %x_hbm.1) | copy-start | bytes 1572868

commit v3 on v2

--- a/solution.py
+++ b/solution.py
@@ -14,9 +14,11 @@
 HEAD_DIM = 128
 BLK = 512
 STEP_ROWS = 8
+LOOP_ROWS = 16
+SKEW = 4
 SLOTS = 7
 FAR_GROUPS = (32, 32)
-OWN_GROUPS = (32, 24, 8)
+OWN_GROUPS = (32, 16, 16)
 F32, BF16 = jnp.float32, jnp.bfloat16
 
 
@@ -197,45 +199,57 @@
     lanes = lax.broadcasted_iota(jnp.int32, (half_heads, 128), 1)
     zero_q = jnp.zeros((2 * half_heads, HEAD_DIM), BF16)
 
+    def scores(b0):
+        bs = [b0, b0 + 1]
+        qf = [jnp.concatenate([q_s[0, b], q_s[1, b]], axis=0) for b in bs]
+        qb = [q.astype(BF16) for q in qf]
+        lhs = jnp.concatenate([jnp.concatenate([qb[0], zero_q], axis=1), jnp.concatenate([zero_q, qb[1]], axis=1)], axis=0)
+        k2 = jnp.concatenate([kv_ref[0, b] for b in bs], axis=1)
+        return qf, lax.dot_general(lhs, k2, (((1,), (1,)), ((), ())), preferred_element_type=F32)
+
+    def weigh(b0, turn, qf, s2):
+        probs, stats = [], []
+        for t in range(2):
+            b = b0 + t
+            at = pos_ref[b] - sp * seq_dev
+            s = s2[t * 2 * half_heads:(t + 1) * 2 * half_heads] * scale
+            old = slots < at
+            here = jnp.logical_and(at >= 0, at < seq_dev)
+            masked = jnp.where(old, s, NEG_FILL)
+            s_new = jnp.sum(qf[t] * kn_ref[pl.ds(b, 1), :], axis=-1, keepdims=True) * scale
+            s_new = jnp.where(here, s_new, NEG_FILL)
+            m = jnp.maximum(jnp.max(masked, axis=-1, keepdims=True), s_new)
+            e = jnp.where(old, jnp.exp(masked - m), 0.0)
+            e_new = jnp.where(here, jnp.exp(s_new - m), 0.0)
+            l = jnp.sum(e, axis=-1, keepdims=True) + e_new
+            probs.append(e.astype(BF16))
+            stats.append((m, l, e_new.astype(BF16).astype(F32) * vn_ref[pl.ds(b, 1), :]))
+        v2 = jnp.concatenate([kv_ref[1, b0 + t] for t in range(2)], axis=1)
+        o2 = jnp.dot(jnp.concatenate(probs, axis=0), v2, preferred_element_type=F32)
+        for t in range(2):
+            m, l, extra = stats[t]
+            o = o2[t * 2 * half_heads:(t + 1) * 2 * half_heads, t * HEAD_DIM:(t + 1) * HEAD_DIM] + extra
+            mb = jnp.broadcast_to(m, o.shape)
+            lb = jnp.broadcast_to(l, o.shape)
+            for f in range(2):
+                hs = slice(f * half_heads, (f + 1) * half_heads)
+                s_loc[f, turn + t, 0] = o[hs]
+                s_loc[f, turn + t, 1] = mb[hs]
+                s_loc[f, turn + t, 2] = lb[hs]
+
     def attend(i, _):
-        k_copy(i).wait()
-        v_copy(i).wait()
-        row = first_row(i)
-        for pair in range(STEP_ROWS // 2):
-            bs = [row + 2 * pair + t for t in range(2)]
-            qf = [jnp.concatenate([q_s[0, b], q_s[1, b]], axis=0) for b in bs]
-            qb = [q.astype(BF16) for q in qf]
-            lhs = jnp.concatenate([jnp.concatenate([qb[0], zero_q], axis=1), jnp.concatenate([zero_q, qb[1]], axis=1)], axis=0)
-            k2 = jnp.concatenate([kv_ref[0, b] for b in bs], axis=1)
-            s2 = lax.dot_general(lhs, k2, (((1,), (1,)), ((), ())), preferred_element_type=F32) * scale
-            probs, stats = [], []
-            for t, b in enumerate(bs):
-                at = pos_ref[b] - sp * seq_dev
-                s = s2[t * 2 * half_heads:(t + 1) * 2 * half_heads]
-                old = slots < at
-                here = jnp.logical_and(at >= 0, at < seq_dev)
-                masked = jnp.where(old, s, NEG_FILL)
-                s_new = jnp.sum(qf[t] * kn_ref[pl.ds(b, 1), :], axis=-1, keepdims=True) * scale
-                s_new = jnp.where(here, s_new, NEG_FILL)
-                m = jnp.maximum(jnp.max(masked, axis=-1, keepdims=True), s_new)
-                e = jnp.where(old, jnp.exp(masked - m), 0.0)
-                e_new = jnp.where(here, jnp.exp(s_new - m), 0.0)
-                l = jnp.sum(e, axis=-1, keepdims=True) + e_new
-                probs.append(e.astype(BF16))
-                stats.append((m, l, e_new.astype(BF16).astype(F32) * vn_ref[pl.ds(b, 1), :]))
-            v2 = jnp.concatenate([kv_ref[1, b] for b in bs], axis=1)
-            o2 = jnp.dot(jnp.concatenate(probs, axis=0), v2, preferred_element_type=F32)
-            for t in range(2):
-                m, l, extra = stats[t]
-                o = o2[t * 2 * half_heads:(t + 1) * 2 * half_heads, t * HEAD_DIM:(t + 1) * HEAD_DIM] + extra
-                mb = jnp.broadcast_to(m, o.shape)
-                lb = jnp.broadcast_to(l, o.shape)
-                turn = i * STEP_ROWS + 2 * pair + t
-                for f in range(2):
-                    hs = slice(f * half_heads, (f + 1) * half_heads)
-                    s_loc[f, turn, 0] = o[hs]
-                    s_loc[f, turn, 1] = mb[hs]
-                    s_loc[f, turn, 2] = lb[hs]
+        per = LOOP_ROWS // STEP_ROWS
+        for c in range(per):
+            k_copy(i * per + c).wait()
+            v_copy(i * per + c).wait()
+        row = first_row(i * per)
+        pairs = LOOP_ROWS // 2
+        ready = {}
+        for n in range(pairs + SKEW):
+            if n < pairs:
+                ready[n] = scores(row + 2 * n)
+            if n >= SKEW:
+                weigh(row + 2 * (n - SKEW), i * LOOP_ROWS + 2 * (n - SKEW), *ready.pop(n - SKEW))
         return 0
 
     sizes = FAR_GROUPS + OWN_GROUPS
@@ -300,7 +314,7 @@
         lax.fori_loop(0, sizes[g] // 8, body, 0)
 
     def run_group(g):
-        lax.fori_loop(starts[g] // STEP_ROWS, (starts[g] + sizes[g]) // STEP_ROWS, attend, 0)
+        lax.fori_loop(starts[g] // LOOP_ROWS, (starts[g] + sizes[g]) // LOOP_ROWS, attend, 0)
         swap_copy(g).start()
 
     def cross_wait(g):
@@ -438,7 +452,7 @@
             dma((6,)), dma, dma, dma((10,)), dma((4,)), dma((n_steps,)), dma((n_steps,)), dma, dma, dma, dma, dma, dma, dma, dma,
             dma((n_all,)), dma((n_all,)), dma((n_far,)), dma((n_far,)), dma((n_far,)), dma((n_far,)), dma((4,)), dma((4,)),
         ],
-        compiler_params=pltpu.CompilerParams(collective_id=0, has_side_effects=True, vmem_limit_bytes=27 << 20),
+        compiler_params=pltpu.CompilerParams(collective_id=0, has_side_effects=True, vmem_limit_bytes=29 << 20),
     )(positions, positions.reshape(1, -1), hidden, ln_gamma.reshape(1, -1), ln_beta.reshape(1, -1), cos_full, sin_full,
       w_qkv, w_up, w_down, w_out, k_cache, v_cache)
 

time: 57.8 us -> 51.2 us (0.89)
  Pallas kernels: 51.2 us -> 44.5 us
  starting transfers between devices: 1.71 us -> 0.03 us
  waiting for transfers between devices: 0.79 us -> 2.44 us
    pallas_call x1, Pallas kernels: 39.3 us -> 32.6 us  [device_step(): pl.pallas_call(layer_kernel, in_specs=[HB] * 13, out_specs=[VM] * 2, out_...]
    ppermute x1, starting transfers between devices: 1.71 us -> 0.03 us  [device_step(): z_far = lax.ppermute(z, 'sp', [(0, 2), (2, 0), (1, 3), (3, 1)])]
    ppermute x1, waiting for transfers between devices: 0.79 us -> 2.44 us  [device_step(): z_far = lax.ppermute(z, 'sp', [(0, 2), (2, 0), (1, 3), (3, 1)])]
  transfers between devices with their start and end apart: 1 -> 1, of which waited for: 1 -> 1; matrix products, arithmetic and copies ran while one was open for 0% -> 0% of each run, Pallas kernels for 21% -> 23%
where the time goes in v3:
time: 51.2 us; the launch traced here: 51.1 us
  Pallas kernels  44.5 us (87%)
  other arithmetic  3.36 us (7%)
  waiting for transfers between devices  2.44 us (5%)
  between operations  0.7 us (1%)
    pallas_call x1, Pallas kernels, device_step(): pl.pallas_call(layer_kernel, in_specs=[HB] * 13, out_specs=[VM] * 2, out_...  32.6 us
    pallas_call x1, Pallas kernels, device_step(): pl.pallas_call(store_kernel, in_specs=[VM], out_specs=[HB, HB], out_shape...  11.9 us
    ppermute x1, waiting for transfers between devices, device_step(): z_far = lax.ppermute(z, 'sp', [(0, 2), (2, 0), (1, 3), (3, 1)])  2.44 us
  transfers between devices with their start and end apart: 1, of which 1 were waited for; matrix products, arithmetic and copies ran while one was open for 0% of the time, Pallas kernels for 23%

profile of v3, /device:TPU:0, one launch (start us, length us, event | category | flops | bytes accessed | tf_op | source)
XLA Modules:
  0.0 51.1 jit_solution(1123092520062431777)
XLA Ops:
  0.6 0.7 %convert_element_type.10 = f32[128]{0:T(128)S(1)} convert(s32[128]{0:T(128)} %pos_hbm) | non-fusion elementwise | flops 128 | bytes 1024 | tf_op jit(solution)/shard_map/convert_element_type | solution.py:27
  1.3 1.0 %fusion.1 = (f32[128,64]{1,0:T(8,128)S(1)}, f32[128,64]{1,0:T(8,128)S(1)}, f32[128,64]{1,0:T(8,128)S(1)}) fusion(f32[64]{0:T(128)} %constant.9, f32[128]{0:T(128)S(1)} %convert_element_type.10), kind=kLoop, calls=%fused_computation.8 | loop fusion | flops 16384 | bytes 99072 | tf_op jit(solution)/shard_map/neg | solution.py:29
  2.3 0.8 %pad_maximum_fusion = (f32[128,128]{1,0:T(8,128)}, f32[128,128]{1,0:T(8,128)}) fusion(f32[128,64]{1,0:T(8,128)S(1)} %get-tuple-element.19, f32[128,64]{1,0:T(8,128)S(1)} %get-tuple-element.18, f32[128,64]{1,0:T(8,128)S(1)} %get-tuple-element.17), kind=kLoop, calls=%fused_computation.6 | loop fusion | flops 32768 | bytes 229376 | tf_op jit(solution)/shard_map/concatenate | solution.py:29
  3.0 32.6 %shard_map.130 = (bf16[2,129,512,128]{3,2,1,0:T(8,128)(2,1)S(1)}, f32[64,2048]{1,0:T(8,128)}) custom-call(s32[128]{0:T(128)} %pos_hbm, s32[1,128]{1,0:T(1,128)} %bitcast.5, bf16[128,2048]{1,0:T(8,128)(2,1)} %x_hbm.1, f32[1,2048]{1,0:T(1,128)} %bitcast.3, f32[1,2048]{1,0:T(1,128)} %bitcast.4, f32[128,128]{1,0:T(8,128)} %get-tuple-element.20.cos_hbm, ...), custom_call_target="tpu_custom_call" | custom-call | tf_op jit(solution)/shard_map/pallas_call | solution.py:432
  35.6 0.0 collective-permute-start
  35.7 0.0 copy-start.1
  35.7 0.0 copy-start
  35.7 11.9 %shard_map.131 = (bf16[128,512,128]{2,1,0:T(8,128)(2,1)}, bf16[128,512,128]{2,1,0:T(8,128)(2,1)}) custom-call(bf16[2,129,512,128]{3,2,1,0:T(8,128)(2,1)S(1)} %get-tuple-element.12.kv_ref), custom_call_target="tpu_custom_call" | custom-call | flops 40000000000 | bytes 33554432 | tf_op jit(solution)/shard_map/pallas_call | solution.py:461
  47.6 2.4 %collective-permute-done = f32[64,2048]{1,0:T(8,128)S(1)} collective-permute-done((f32[64,2048]{1,0:T(8,128)}, f32[64,2048]{1,0:T(8,128)S(1)}, u32[]{:S(2)}, u32[]{:S(2)}) %collective-permute-start) | collective-permute-done | bytes 524320 | tf_op jit(solution)/shard_map/ppermute | solution.py:459
  50.1 0.0 copy-done.1
  50.1 0.1 broadcast_select_fusion.1
  50.2 0.0 copy-done
  50.2 0.9 %fusion = bf16[128,2048]{1,0:T(8,128)(2,1)} fusion(f32[64,2048]{1,0:T(8,128)S(1)} %get-tuple-element.16, f32[64,2048]{1,0:T(8,128)S(1)} %get-tuple-element.15, bf16[128,2048]{1,0:T(8,128)(2,1)S(1)} %copy-done), kind=kLoop, calls=%fused_computation.1 | loop fusion | flops 1048576 | bytes 2097152 | tf_op jit(solution)/shard_map/convert_element_type | solution.py:474
Async XLA Ops:
  35.6 14.4 %collective-permute-start = (f32[64,2048]{1,0:T(8,128)}, f32[64,2048]{1,0:T(8,128)S(1)}, u32[]{:S(2)}, u32[]{:S(2)}) collective-permute-start(f32[64,2048]{1,0:T(8,128)} %get-tuple-element.11), channel_id=1, source_target_pairs={{0,2},{2,0},{1,3},{3,1},{4,6},{6,4},{5,7},{7,5}} | collective-permute-start | bytes 1572872 | tf_op jit(solution)/shard_map/ppermute | solution.py:459
  35.7 14.4 %copy-start.1 = (f32[64,2048]{1,0:T(8,128)S(1)}, f32[64,2048]{1,0:T(8,128)}, u32[]{:S(2)}) copy-start(f32[64,2048]{1,0:T(8,128)} %get-tuple-element.11) | copy-start | bytes 1572868
  35.7 14.5 %copy-start = (bf16[128,2048]{1,0:T(8,128)(2,1)S(1)}, bf16[128,2048]{1,0:T(8,128)(2,1)}, u32[]{:S(2)}) copy-start(bf16[128,2048]{1,0:T(8,128)(2,1)} %x_hbm.1) | copy-start | bytes 1572868

commit v4 on v3

--- a/solution.py
+++ b/solution.py
@@ -17,21 +17,19 @@
 LOOP_ROWS = 16
 SKEW = 4
 SLOTS = 7
-FAR_GROUPS = (32, 32)
+FAR_GROUPS = (16, 16, 16, 16)
 OWN_GROUPS = (32, 16, 16)
 F32, BF16 = jnp.float32, jnp.bfloat16
 
 
-def rope_tables(positions):
+def rope_rates():
     inv_freq = (ROPE_BASE ** (-np.arange(0, HEAD_DIM, 2) / HEAD_DIM)).astype(np.float32)
-    angles = positions.astype(F32)[:, None] * inv_freq[None, :]
-    cos_half, sin_half = jnp.cos(angles), jnp.sin(angles)
-    return jnp.concatenate([cos_half, cos_half], axis=-1), jnp.concatenate([-sin_half, sin_half], axis=-1)
-
-
-def layer_kernel(pos_hbm, posv_hbm, x_hbm, gamma_hbm, beta_hbm, cos_hbm, sin_hbm, wqkv_hbm, wup_hbm, wdown_hbm, wout_hbm,
+    return np.concatenate([inv_freq, inv_freq])[None, :]
+
+
+def layer_kernel(pos_hbm, posv_hbm, x_hbm, gamma_hbm, beta_hbm, rate_hbm, wqkv_hbm, wup_hbm, wdown_hbm, wout_hbm,
                  k_hbm, v_hbm, kv_ref, z_ref,
-                 pos_ref, posv_ref, gamma_ref, beta_ref, cos_ref, sin_ref,
+                 pos_ref, posv_ref, gamma_ref, beta_ref, rate_ref, cos_ref, sin_ref,
                  xbuf, hbuf, kvw, wbuf, q_s, kn_ref, vn_ref, act, ctx_ref, part, mrecv, mx_recv, mlp_own, mlp_mate, arecv,
                  s_loc, s_recv, chip_o, chip_ml, x_o, x_ml,
                  insem, xsem, kvwsem, wsem, osem, ksem, vsem, q_ss, q_rs, m_ss, m_rs, mx_ss, mx_rs, mm_ss, mm_rs,
@@ -43,7 +41,6 @@
     across = (dp, lax.rem(sp + 2, 4))
     rows = xbuf.shape[0]
     own_rows = rows // 2
-    n_steps = rows // STEP_ROWS
     seq_dev = k_hbm.shape[1]
     half_heads = q_s.shape[2]
     half_cols = half_heads * HEAD_DIM
@@ -55,14 +52,14 @@
         return pltpu.make_async_copy(src.at[:, pl.ds(pl.multiple_of(col, BLK), BLK)], wbuf.at[slot], wsem.at[idx])
 
     def q_copy(j):
-        return weight_copy(wqkv_hbm, core * half_cols + j * BLK, j, j)
+        return weight_copy(wqkv_hbm, core * half_cols + j * BLK, 1 + j, 8 + j)
 
     def up_copy(j):
-        return weight_copy(wup_hbm, j * BLK, 2 + j, 2 + j)
+        return weight_copy(wup_hbm, j * BLK, j, j)
 
     def down_copy(j):
         half = jnp.where(j < 2, 1 - core, core)
-        return weight_copy(wdown_hbm, half * half_cols + lax.rem(j, 2) * BLK, lax.rem(6 + j, SLOTS), 6 + j)
+        return weight_copy(wdown_hbm, half * half_cols + lax.rem(j, 2) * BLK, lax.rem(4 + j, SLOTS), 4 + j)
 
     def out_copy(j):
         half = (1 - core) if j < 2 else core
@@ -88,17 +85,16 @@
     x_copy = pltpu.make_async_copy(x_hbm, xbuf, xsem)
     x_copy.start()
     small = [pltpu.make_async_copy(src, dst, insem.at[n]) for n, (src, dst) in enumerate((
-        (gamma_hbm, gamma_ref), (beta_hbm, beta_ref), (cos_hbm, cos_ref), (sin_hbm, sin_ref), (posv_hbm, posv_ref),
+        (gamma_hbm, gamma_ref), (beta_hbm, beta_ref), (rate_hbm, rate_ref), (posv_hbm, posv_ref),
         (pos_hbm, pos_ref)))]
     for copy in small:
         copy.start()
+    for j in range(4):
+        up_copy(j).start()
+    for j in range(3):
+        down_copy(j).start()
     kvw_copy = pltpu.make_async_copy(wqkv_hbm.at[:, pl.ds(2 * half_cols, 2 * HEAD_DIM)], kvw, kvwsem)
     kvw_copy.start()
-    for j in range(2):
-        q_copy(j).start()
-    for j in range(4):
-        up_copy(j).start()
-    down_copy(0).start()
 
     barrier = pltpu.get_barrier_semaphore()
     for dev in (mate, across):
@@ -120,10 +116,60 @@
 
     lax.fori_loop(0, rows // 32, norm_rows, 0)
 
+    turns = jnp.broadcast_to(posv_ref[...], (HEAD_DIM, rows)).astype(F32).T * rate_ref[...]
+    lane = lax.broadcasted_iota(jnp.int32, (rows, HEAD_DIM), 1)
+    cos_ref[...] = jnp.cos(turns)
+    sin_ref[...] = jnp.where(lane < HEAD_DIM // 2, -jnp.sin(turns), jnp.sin(turns))
+
     def rotate(vec):
         vec = vec.astype(BF16).astype(F32)
         return (vec * cos_ref[...] + pltpu.roll(vec, HEAD_DIM // 2, 1) * sin_ref[...]).astype(BF16)
 
+    def up_step(j, _):
+        up_copy(j).wait()
+        for n in range(2):
+            up = jnp.dot(hbuf[...], wbuf[j, :, n * 256:(n + 1) * 256], preferred_element_type=F32)
+            gelu = 0.5 * up * (1.0 + lax.erf(up * (0.5 ** 0.5)))
+            act[:, pl.ds(pl.multiple_of(j * BLK + n * 256, 256), 256)] = gelu.astype(BF16)
+
+        @pl.when(j == 0)
+        def _():
+            down_copy(3).start()
+
+        @pl.when(j == 1)
+        def _():
+            q_copy(0).start()
+
+        @pl.when(j == 2)
+        def _():
+            q_copy(1).start()
+
+        @pl.when(j == 3)
+        def _():
+            cache_start(0)
+            cache_start(1)
+
+        return 0
+
+    lax.fori_loop(0, 4, up_step, 0)
+
+    def down_step(j, _):
+        down_copy(j).wait()
+        slot = lax.rem(4 + j, SLOTS)
+        for n in range(2):
+            part[j // 2, :, pl.ds(pl.multiple_of(lax.rem(j, 2) * BLK + n * 256, 256), 256)] = jnp.dot(
+                act[...], wbuf[slot, :, n * 256:(n + 1) * 256], preferred_element_type=F32)
+        cache_start(2 + 2 * j)
+        cache_start(3 + 2 * j)
+        return 0
+
+    m_send = pltpu.make_async_remote_copy(src_ref=part.at[0], dst_ref=mrecv, send_sem=m_ss, recv_sem=m_rs,
+                                          device_id=mate, device_id_type=MESH)
+    lax.fori_loop(0, 2, down_step, 0)
+    m_send.start()
+    lax.fori_loop(2, 4, down_step, 0)
+    for j in range(4):
+        out_copy(j).start()
     kvw_copy.wait()
     kv_new = jnp.dot(hbuf[...], kvw[...], preferred_element_type=F32)
     k_new = rotate(kv_new[:, :HEAD_DIM])
@@ -138,61 +184,23 @@
     kv_ref[0, rows, rows:rows + 16, :] = tile.astype(F32).astype(BF16)
     kv_ref[0, rows, rows + 16:rows + 32, :] = jnp.where(inside, at - tile * 16, 16).astype(F32).astype(BF16)
 
-    for j in range(2):
-        q_copy(j).wait()
-        for n in range(2):
-            q_part = jnp.dot(hbuf[...], wbuf[j, :, n * 256:(n + 1) * 256], preferred_element_type=F32)
-            for t in range(2):
-                q_s[core, :, j * 4 + n * 2 + t, :] = rotate(q_part[:, t * HEAD_DIM:(t + 1) * HEAD_DIM]).astype(F32)
-        down_copy(1 + j).start()
-    q_send = pltpu.make_async_remote_copy(src_ref=q_s.at[core], dst_ref=q_s.at[core], send_sem=q_ss, recv_sem=q_rs,
-                                          device_id=mate, device_id_type=MESH)
-    q_send.start()
-
-    def up_step(j, _):
-        up_copy(j).wait()
-        for n in range(2):
-            up = jnp.dot(hbuf[...], wbuf[2 + j, :, n * 256:(n + 1) * 256], preferred_element_type=F32)
-            gelu = 0.5 * up * (1.0 + lax.erf(up * (0.5 ** 0.5)))
-            act[:, pl.ds(pl.multiple_of(j * BLK + n * 256, 256), 256)] = gelu.astype(BF16)
-
-        @pl.when(j == 0)
-        def _():
-            down_copy(3).start()
-            cache_start(0)
-
-        @pl.when(j > 0)
-        def _():
-            cache_start(2 * j - 1)
-            cache_start(2 * j)
-
-        return 0
-
-    lax.fori_loop(0, 4, up_step, 0)
-
-    def down_step(j, _):
-        down_copy(j).wait()
-        slot = lax.rem(6 + j, SLOTS)
-        for n in range(2):
-            part[j // 2, :, pl.ds(pl.multiple_of(lax.rem(j, 2) * BLK + n * 256, 256), 256)] = jnp.dot(
-                act[...], wbuf[slot, :, n * 256:(n + 1) * 256], preferred_element_type=F32)
-        cache_start(7 + 2 * j)
-        cache_start(8 + 2 * j)
-        return 0
-
-    m_send = pltpu.make_async_remote_copy(src_ref=part.at[0], dst_ref=mrecv, send_sem=m_ss, recv_sem=m_rs,
-                                          device_id=mate, device_id_type=MESH)
-    lax.fori_loop(0, 2, down_step, 0)
-    m_send.start()
-    lax.fori_loop(2, 4, down_step, 0)
-    cache_start(n_steps - 1)
-    for j in range(4):
-        out_copy(j).start()
     m_send.wait()
     part[1] = part[1] + mrecv[...]
     mx_send = pltpu.make_async_remote_copy(src_ref=part.at[1, pl.ds(far_base, own_rows)], dst_ref=mx_recv, send_sem=mx_ss,
                                            recv_sem=mx_rs, device_id=across, device_id_type=MESH)
     mx_send.start()
+    for j in range(2):
+        q_copy(j).wait()
+        for n in range(2):
+            q_part = jnp.dot(hbuf[...], wbuf[1 + j, :, n * 256:(n + 1) * 256], preferred_element_type=F32)
+            for t in range(2):
+                q_s[core, :, j * 4 + n * 2 + t, :] = rotate(q_part[:, t * HEAD_DIM:(t + 1) * HEAD_DIM]).astype(F32)
+        for c in range(3):
+            cache_start(10 + 3 * j + c)
+    q_send = pltpu.make_async_remote_copy(src_ref=q_s.at[core], dst_ref=q_s.at[core], send_sem=q_ss, recv_sem=q_rs,
+                                          device_id=mate, device_id_type=MESH)
+    q_send.start()
+
     q_send.wait()
 
     slots = lax.broadcasted_iota(jnp.int32, (2 * half_heads, seq_dev), 1)
@@ -299,9 +307,8 @@
             for u in range(8):
                 b = starts[g] + i * 8 + u
                 src = b - own_rows
-                part_g = starts[g] - own_rows
-                xg = [n for n in range(n_far) if starts[n] <= part_g][-1]
-                hit = lanes == src - starts[xg]
+                xg = lax.div(src, FAR_GROUPS[0])
+                hit = lanes == lax.rem(src, FAR_GROUPS[0])
                 m_x = jnp.sum(jnp.where(hit, x_ml[xg, 0], 0.0), axis=-1, keepdims=True)
                 l_x = jnp.sum(jnp.where(hit, x_ml[xg, 1], 0.0), axis=-1, keepdims=True)
                 m_a, m_b = s_loc[core, b, 1], s_recv[b, 1]
@@ -323,21 +330,19 @@
 
     mm_send = pltpu.make_async_remote_copy(src_ref=mlp_own, dst_ref=mlp_mate, send_sem=mm_ss, recv_sem=mm_rs,
                                            device_id=mate, device_id_type=MESH)
-    run_group(0)
-    run_group(1)
-    merge_far(0)
-    run_group(2)
-    merge_far(1)
-    run_group(3)
+    for g in range(n_far + 1):
+        run_group(g)
+        if g > 0:
+            merge_far(g - 1)
+    run_group(n_far + 1)
     mx_send.wait()
     mlp_own[...] = part[1, pl.ds(own_base, own_rows), :] + mx_recv[...]
     mm_send.start()
-    run_group(4)
-    cross_wait(0)
-    merge_own(2)
-    cross_wait(1)
-    merge_own(3)
-    merge_own(4)
+    run_group(n_far + 2)
+    for g in range(n_far):
+        cross_wait(g)
+    for g in range(n_far, len(sizes)):
+        merge_own(g)
     for h in range(half_heads):
         ctx_ref[:, h * HEAD_DIM:(h + 1) * HEAD_DIM] = x_o[:, h, :].astype(BF16)
     mm_send.wait()
@@ -426,17 +431,16 @@
     own_rows = rows // 2
     n_steps, n_far, n_all = rows // STEP_ROWS, len(FAR_GROUPS), len(FAR_GROUPS) + len(OWN_GROUPS)
     positions, upper = lax.optimization_barrier((positions, lax.axis_index('sp') < 2))
-    cos_full, sin_full = rope_tables(positions)
     dma = pltpu.SemaphoreType.DMA
     heads_f32 = (half_heads, HEAD_DIM)
     kv, z = pl.pallas_call(
         layer_kernel,
-        in_specs=[HB] * 13,
+        in_specs=[HB] * 12,
         out_specs=[VM] * 2,
         out_shape=[pltpu.VMEM((2, rows + 1) + k_cache.shape[1:], BF16), jax.ShapeDtypeStruct((own_rows, d_model), F32)],
         scratch_shapes=[
             pltpu.SMEM((rows,), jnp.int32), pltpu.VMEM((1, rows), jnp.int32),
-            pltpu.VMEM((1, d_model), F32), pltpu.VMEM((1, d_model), F32),
+            pltpu.VMEM((1, d_model), F32), pltpu.VMEM((1, d_model), F32), pltpu.VMEM((1, HEAD_DIM), F32),
             pltpu.VMEM((rows, HEAD_DIM), F32), pltpu.VMEM((rows, HEAD_DIM), F32),
             pltpu.VMEM((rows, d_model), BF16), pltpu.VMEM((rows, d_model), BF16),
             pltpu.VMEM((d_model, 2 * HEAD_DIM), BF16), pltpu.VMEM((SLOTS, d_model, BLK), BF16),
@@ -449,11 +453,11 @@
             pltpu.VMEM((2, rows, 3) + heads_f32, F32), pltpu.VMEM((rows, 3) + heads_f32, F32),
             pltpu.VMEM((own_rows,) + heads_f32, F32), pltpu.VMEM((n_far, 2) + heads_f32, F32),
             pltpu.VMEM((own_rows,) + heads_f32, F32), pltpu.VMEM((n_far, 2) + heads_f32, F32),
-            dma((6,)), dma, dma, dma((10,)), dma((4,)), dma((n_steps,)), dma((n_steps,)), dma, dma, dma, dma, dma, dma, dma, dma,
+            dma((5,)), dma, dma, dma((10,)), dma((4,)), dma((n_steps,)), dma((n_steps,)), dma, dma, dma, dma, dma, dma, dma, dma,
             dma((n_all,)), dma((n_all,)), dma((n_far,)), dma((n_far,)), dma((n_far,)), dma((n_far,)), dma((4,)), dma((4,)),
         ],
         compiler_params=pltpu.CompilerParams(collective_id=0, has_side_effects=True, vmem_limit_bytes=29 << 20),
-    )(positions, positions.reshape(1, -1), hidden, ln_gamma.reshape(1, -1), ln_beta.reshape(1, -1), cos_full, sin_full,
+    )(positions, positions.reshape(1, -1), hidden, ln_gamma.reshape(1, -1), ln_beta.reshape(1, -1), rope_rates(),
       w_qkv, w_up, w_down, w_out, k_cache, v_cache)
 
     z_far = lax.ppermute(z, 'sp', [(0, 2), (2, 0), (1, 3), (3, 1)])

time: 51.2 us -> 48.4 us (0.945)
  other arithmetic: 3.36 us -> 0.98 us
    neg x1 -> x0, other arithmetic: 0.96 us -> none  [rope_tables(): -sin_half]
    concatenate x1 -> x0, other arithmetic: 0.76 us -> none  [rope_tables(): jnp.concatenate([cos_half, cos_half], axis=-1)]
    convert_element_type x1 -> x0, other arithmetic: 0.66 us -> none  [rope_tables(): angles = positions.astype(F32)[:, None] * inv_freq[None, :]]
  transfers between devices with their start and end apart: 1 -> 1, of which waited for: 1 -> 1; matrix products, arithmetic and copies ran while one was open for 0% -> 0% of each run, Pallas kernels for 23% -> 25%
where the time goes in v4:
time: 48.4 us; the launch traced here: 48.3 us
  Pallas kernels  44.1 us (91%)
  waiting for transfers between devices  2.44 us (5%)
  other arithmetic  0.98 us (2%)
  between operations  0.7 us (1%)
    pallas_call x1, Pallas kernels, device_step(): pl.pallas_call(layer_kernel, in_specs=[HB] * 12, out_specs=[VM] * 2, out_...  32.2 us
    pallas_call x1, Pallas kernels, device_step(): pl.pallas_call(store_kernel, in_specs=[VM], out_specs=[HB, HB], out_shape...  11.9 us
    ppermute x1, waiting for transfers between devices, device_step(): z_far = lax.ppermute(z, 'sp', [(0, 2), (2, 0), (1, 3), (3, 1)])  2.44 us
  transfers between devices with their start and end apart: 1, of which 1 were waited for; matrix products, arithmetic and copies ran while one was open for 0% of the time, Pallas kernels for 25%

profile of v4, /device:TPU:0, one launch (start us, length us, event | category | flops | bytes accessed | tf_op | source)
XLA Modules:
  0.0 48.3 jit_solution(10526049896738237516)
XLA Ops:
  0.6 32.2 %shard_map.130 = (bf16[2,129,512,128]{3,2,1,0:T(8,128)(2,1)S(1)}, f32[64,2048]{1,0:T(8,128)}) custom-call(s32[128]{0:T(128)} %pos_hbm, s32[1,128]{1,0:T(1,128)} %bitcast.5, bf16[128,2048]{1,0:T(8,128)(2,1)} %x_hbm.1, f32[1,2048]{1,0:T(1,128)} %bitcast.3, f32[1,2048]{1,0:T(1,128)} %bitcast.4, f32[1,128]{1,0:T(1,128)} %constant.8.clone.rate_hbm, ...), custom_call_target="tpu_custom_call" | custom-call | tf_op jit(solution)/shard_map/pallas_call | solution.py:436
  32.9 0.0 collective-permute-start
  32.9 0.0 copy-start.1
  32.9 0.0 copy-start
  32.9 11.9 %shard_map.131 = (bf16[128,512,128]{2,1,0:T(8,128)(2,1)}, bf16[128,512,128]{2,1,0:T(8,128)(2,1)}) custom-call(bf16[2,129,512,128]{3,2,1,0:T(8,128)(2,1)S(1)} %get-tuple-element.12.kv_ref), custom_call_target="tpu_custom_call" | custom-call | flops 40000000000 | bytes 33554432 | tf_op jit(solution)/shard_map/pallas_call | solution.py:465
  44.8 2.4 %collective-permute-done = f32[64,2048]{1,0:T(8,128)S(1)} collective-permute-done((f32[64,2048]{1,0:T(8,128)}, f32[64,2048]{1,0:T(8,128)S(1)}, u32[]{:S(2)}, u32[]{:S(2)}) %collective-permute-start) | collective-permute-done | bytes 524320 | tf_op jit(solution)/shard_map/ppermute | solution.py:463
  47.3 0.0 copy-done.1
  47.3 0.1 broadcast_select_fusion.1
  47.4 0.0 copy-done
  47.4 0.9 %fusion = bf16[128,2048]{1,0:T(8,128)(2,1)} fusion(f32[64,2048]{1,0:T(8,128)S(1)} %get-tuple-element.16, f32[64,2048]{1,0:T(8,128)S(1)} %get-tuple-element.15, bf16[128,2048]{1,0:T(8,128)(2,1)S(1)} %copy-done), kind=kLoop, calls=%fused_computation.1 | loop fusion | flops 1048576 | bytes 2097152 | tf_op jit(solution)/shard_map/convert_element_type | solution.py:478
Async XLA Ops:
  32.9 14.4 %collective-permute-start = (f32[64,2048]{1,0:T(8,128)}, f32[64,2048]{1,0:T(8,128)S(1)}, u32[]{:S(2)}, u32[]{:S(2)}) collective-permute-start(f32[64,2048]{1,0:T(8,128)} %get-tuple-element.11), channel_id=1, source_target_pairs={{0,2},{2,0},{1,3},{3,1},{4,6},{6,4},{5,7},{7,5}} | collective-permute-start | bytes 1572872 | tf_op jit(solution)/shard_map/ppermute | solution.py:463
  32.9 14.4 %copy-start.1 = (f32[64,2048]{1,0:T(8,128)S(1)}, f32[64,2048]{1,0:T(8,128)}, u32[]{:S(2)}) copy-start(f32[64,2048]{1,0:T(8,128)} %get-tuple-element.11) | copy-start | bytes 1572868
  32.9 14.5 %copy-start = (bf16[128,2048]{1,0:T(8,128)(2,1)S(1)}, bf16[128,2048]{1,0:T(8,128)(2,1)}, u32[]{:S(2)}) copy-start(bf16[128,2048]{1,0:T(8,128)(2,1)} %x_hbm.1) | copy-start | bytes 1572868
